TPU v7x, 128 devices: a whole 4x4x4 slice. The times are simulated.
128 devices in a mesh: band: 32 (over y, x, core), lev: 4 (over z).
Axes of the slice: x: 4, y: 4, z: 4, core: 2. Of those that a mesh axis runs over, the one named last changes fastest.
Arguments:
- field_grid: float32 [3, 16, 384, 2, 1536], P(None, 'lev', 'band'), may hold values from -6 to 6
- increment: float32 [3, 16, 384, 2, 1536], P(None, 'lev', 'band'), may hold values from -6 to 6
- points: int32 [384], P('band'), may hold values from 16 to 1536, as said below
- weights: float32 [384], replicated, may hold values from 0.0013020834 to 0.0052083335
- pair_slot: int32 [384], replicated, may hold values from 0 to 383, each once
- legendre: float32 [384, 384, 769], P(('band', 'lev')), may hold values from -6 to 6
- strength: float32 [3, 16], replicated, may hold values from 1 to 16
Outputs:
- stepped: float32 [3, 16, 384, 2, 1536], P(None, 'lev', 'band')
Inputs may be any that keep to these rules, and one draw needn't show every extreme that they name: points[j] lies within 32 of 16 + 1520 * j // 383, kept within 16 to 1536; the last latitude pair has 1536 cells. `pair_slot`: A permutation of 0 to 383; slot s is held by the device of joint band+lev index s // 3, at place s % 3, which holds legendre[s].
All inputs are finite; a program needn't handle non-finite values.
Results may differ from a plain program's by a relative error of at most 0.0003.
Values sent between devices are 32-bit elements; how exact they have to be, the bound alone decides.
A program may use at most 128 MiB of HBM per device.

v0:
```python
import math

import jax
import jax.numpy as jnp
from jax import lax
from jax.sharding import PartitionSpec as P

TWO_PI = 2.0 * math.pi


def cut_along(value, dim, size):
    before, after = (value.shape[:dim], value.shape[dim + 1 :])
    return jnp.moveaxis(value.reshape(*before, size, -1, *after), dim, 0)


def joined_along(blocks, dim):
    lengths = list(blocks.shape[1:])
    lengths[dim] *= blocks.shape[0]
    return jnp.moveaxis(blocks, 0, dim).reshape(lengths)


def one_exchange(value, axis, axes, splits, concats):
    sizes = [lax.axis_size(a) for a in axes]
    blocks = cut_along(value, splits[0], sizes[0])
    blocks = jnp.moveaxis(cut_along(blocks, splits[1] + 1, sizes[1]), 0, 1)
    inside = blocks.shape[2:]
    blocks = blocks.reshape(-1, *inside)
    blocks = lax.all_to_all(blocks, axis, split_axis=0, concat_axis=0, tiled=True)
    blocks = joined_along(blocks.reshape(*sizes, *inside), concats[0] + 1)
    return joined_along(blocks, concats[1])


def dft_tables(counts, length, wavecount):
    inner = 32
    outer = length // inner
    orders = lax.iota(jnp.int32, wavecount)
    coarse = lax.iota(jnp.int32, outer) * inner
    finer = lax.iota(jnp.int32, inner)
    modulus = counts[:, None, None]
    step_angle = (TWO_PI / counts.astype(jnp.float32))[:, None, None]
    coarse_angle = (coarse[None, :, None] * orders[None, None, :] % modulus).astype(
        jnp.float32
    ) * step_angle
    finer_angle = (finer[None, :, None] * orders[None, None, :] % modulus).astype(
        jnp.float32
    ) * step_angle
    coarse_cos = jnp.cos(coarse_angle)[:, :, None, :]
    coarse_sin = jnp.sin(coarse_angle)[:, :, None, :]
    finer_cos = jnp.cos(finer_angle)[:, None, :, :]
    finer_sin = jnp.sin(finer_angle)[:, None, :, :]
    pair_count = counts.shape[0]
    full_cos = (coarse_cos * finer_cos - coarse_sin * finer_sin).reshape(
        pair_count, length, wavecount
    )
    full_sin = (coarse_sin * finer_cos + coarse_cos * finer_sin).reshape(
        pair_count, length, wavecount
    )
    places = lax.iota(jnp.int32, length)
    live = (places[None, :, None] < modulus) & (orders[None, None, :] <= (modulus - 1) // 2)
    cosines = jnp.where(live, full_cos, 0.0)
    sines = jnp.where(live, -full_sin, 0.0)
    return jnp.concatenate([cosines, sines], axis=2)


def body(field_grid, increment, points, weights, pair_slot, legendre, strength):
    band_count = lax.axis_size("band")
    level_groups = lax.axis_size("lev")
    summed = field_grid + increment
    fields = summed.shape[0]
    local_levels = summed.shape[1]
    band_pairs = summed.shape[2]
    length = summed.shape[4]
    wavecount = length // 2
    pair_total = wavecount // 2
    total_levels = local_levels * level_groups
    regrouped = lax.all_to_all(summed, "lev", split_axis=2, concat_axis=1, tiled=True)
    piece_pairs = band_pairs // level_groups
    counts = lax.dynamic_slice_in_dim(points, lax.axis_index("lev") * piece_pairs, piece_pairs)
    tables = dft_tables(counts, length, wavecount)
    row_count = fields * total_levels * 2
    pair_rows = jnp.moveaxis(regrouped, 2, 0).reshape(piece_pairs, row_count, length)
    spectra = jnp.einsum("pqx,pxk->pqk", pair_rows, tables, precision=lax.Precision.HIGHEST)
    spectra = spectra / counts.astype(jnp.float32)[:, None, None]
    piece_width = 2 * row_count
    by_wave = jnp.transpose(spectra.reshape(piece_pairs, row_count, 2, wavecount), (3, 0, 2, 1))
    by_wave = by_wave.reshape(wavecount, piece_pairs, piece_width)
    slot_ranks = lax.iota(jnp.int32, pair_total)
    pair_of_slot = jnp.zeros((pair_total,), jnp.int32).at[pair_slot].set(slot_ranks)
    wave_order = jnp.stack([pair_of_slot, wavecount - 1 - pair_of_slot], axis=1).reshape(wavecount)
    outgoing = jnp.take(by_wave, wave_order, axis=0)
    slot_count = legendre.shape[0]
    sectioned = outgoing.reshape(
        band_count, level_groups, 2 * slot_count, 1, 1, piece_pairs, piece_width
    )
    arrived = one_exchange(sectioned, ("band", "lev"), ("band", "lev"), (0, 1), (3, 4))
    arrived = arrived.reshape(2 * slot_count, band_count, level_groups, piece_pairs, piece_width)
    row_width = 4 * fields * total_levels
    arrived = arrived.reshape(2 * slot_count, pair_total, row_width)
    lat_count = arrived.shape[1]
    own_slots = lax.axis_index(("band", "lev")) * slot_count + lax.iota(jnp.int32, slot_count)
    lower_wave = jnp.take(pair_of_slot, own_slots)
    columns = lax.iota(jnp.int32, wavecount + 1)
    second_member = columns[None, :] >= (wavecount - lower_wave)[:, None]
    degree = jnp.where(second_member, columns[None, :] - 1, lower_wave[:, None] + columns[None, :])
    wave_of_column = jnp.where(
        second_member, wavecount - 1 - lower_wave[:, None], lower_wave[:, None]
    )
    parity = jnp.where((degree - wave_of_column) % 2 == 0, 1.0, -1.0)
    weighted = arrived.reshape(slot_count, 2, lat_count, row_width) * weights[None, None, :, None]
    analysed = jnp.einsum("sjc,sejr->scer", legendre, weighted, precision=lax.Precision.HIGHEST)
    analysed = analysed.reshape(slot_count, wavecount + 1, 2, 2, fields * total_levels, 2)
    chosen = jnp.where(second_member[:, :, None, None, None], analysed[:, :, 1], analysed[:, :, 0])
    coefficients = chosen[..., 0] + parity[:, :, None, None] * chosen[..., 1]
    degree_real = degree.astype(jnp.float32)
    degree_ratio = degree_real * (degree_real + 1.0) / float((wavecount - 1) * wavecount)
    damping_rate = strength.reshape(fields * total_levels)
    damping = 1.0 / (1.0 + damping_rate[None, None, :] * (degree_ratio * degree_ratio)[:, :, None])
    damped = coefficients * damping[:, :, None, :]
    second_real = jnp.where(second_member, 1.0, 0.0)
    member_mask = jnp.stack([1.0 - second_real, second_real], axis=2)
    hemisphere_sign = jnp.stack([jnp.ones_like(parity), parity], axis=2)
    spread = damped[:, :, None, :, :, None] * member_mask[:, :, :, None, None, None]
    spread = spread * hemisphere_sign[:, :, None, None, None, :]
    spread = spread.reshape(slot_count, wavecount + 1, 2 * row_width)
    returned = jnp.einsum("sjc,scr->sjr", legendre, spread, precision=lax.Precision.HIGHEST)
    leaving = jnp.transpose(returned.reshape(slot_count, lat_count, 2, row_width), (0, 2, 1, 3))
    leaving = leaving.reshape(2 * slot_count, lat_count, row_width)
    leaving = leaving.reshape(2 * slot_count, band_count, level_groups, piece_pairs, piece_width)
    sectioned_back = leaving.reshape(
        1, 1, 2 * slot_count, band_count, level_groups, piece_pairs, piece_width
    )
    home_rows = one_exchange(sectioned_back, ("band", "lev"), ("band", "lev"), (3, 4), (0, 1))
    home_rows = home_rows.reshape(wavecount, piece_pairs, piece_width)
    positions = (
        jnp.zeros((wavecount,), jnp.int32).at[wave_order].set(lax.iota(jnp.int32, wavecount))
    )
    restored = jnp.take(home_rows, positions, axis=0)
    spectral_rows = jnp.transpose(
        restored.reshape(wavecount, piece_pairs, 2, row_count), (1, 3, 2, 0)
    )
    spectral_rows = spectral_rows.reshape(piece_pairs, row_count, 2 * wavecount)
    doubling = jnp.where(lax.iota(jnp.int32, 2 * wavecount) % wavecount == 0, 1.0, 2.0)
    grid_rows = jnp.einsum(
        "pqk,pxk->pqx",
        spectral_rows * doubling[None, None, :],
        tables,
        precision=lax.Precision.HIGHEST,
    )
    grid_rows = jnp.moveaxis(grid_rows.reshape(piece_pairs, fields, total_levels, 2, length), 0, 2)
    return lax.all_to_all(grid_rows, "lev", split_axis=1, concat_axis=2, tiled=True)


def solution(mesh):
    return jax.shard_map(
        body,
        mesh=mesh,
        in_specs=(
            P(None, "lev", "band", None, None),
            P(None, "lev", "band", None, None),
            P("band"),
            P(),
            P(),
            P(("band", "lev"), None, None),
            P(),
        ),
        out_specs=P(None, "lev", "band", None, None),
        check_vma=False,
    )
```

profile of v0, /device:TPU:1, one launch (start us, length us, event | category | flops | bytes accessed | tf_op | source)
XLA Modules:
  0.0 308.7 jit_solution(86168161604237472)
XLA Ops:
  0.0 4.3 %copy_add_fusion = f32[3,4,12,2,1536]{4,3,1,0,2:T(2,128)} fusion(f32[3,4,12,2,1536]{4,3,2,1,0:T(2,128)} %param.10, f32[3,4,12,2,1536]{4,3,2,1,0:T(2,128)} %param.9), kind=kLoop, calls=%fused_computation.24 | loop fusion | flops 442368 | bytes 5308416 | tf_op jit(solution)/shard_map/add | solution.py:68
  4.3 6.0 %all-to-all-start = ((f32[3,4,12,2,1536]{4,3,1,0,2:T(2,128)}), f32[3,4,12,2,1536]{4,3,1,0,2:T(2,128)S(1)}, u32[]{:S(2)}, u32[]{:S(2)}) async-start(f32[3,4,12,2,1536]{4,3,1,0,2:T(2,128)} %copy_add_fusion), calls=%async_computation | async-start | bytes 3538944 | tf_op jit(solution)/shard_map/all_to_all | solution.py:76
  10.5 3.1 %scatter_custom_fusion = s32[384]{0:T(512)S(1)} fusion(s32[384]{0:T(512)S(1)} %compare_select_fusion.7, s32[384]{0:T(512)S(1)} %iota.105, s32[]{:T(128)} %constant.72.clone.1), kind=kCustom, calls=%fused_computation.110 | custom fusion | bytes 1540 | tf_op jit(solution)/shard_map/scatter | solution.py:88
  14.1 0.4 copy-done.3
  14.5 5.8 %fusion.19 = (f32[3,48,768]{2,1,0:T(8,128)S(1)}, f32[3,48,768]{2,1,0:T(8,128)S(1)}) fusion(f32[3]{0:T(128)S(1)} %broadcast_divide_fusion, s32[3]{0:T(128)S(1)} %get-tuple-element.26, s32[48,768]{1,0:T(8,128)S(1)} %iota_multiply_fusion, pred[3]{0:T(512)(128)(4,1)S(1)} %broadcast_compare_fusion), kind=kLoop, calls=%fused_computation.48 | loop fusion | flops 995328 | bytes 1032219 | tf_op jit(solution)/shard_map/cos | solution.py:47
  20.3 3.9 %fusion.25 = (f32[3,32,768]{2,1,0:T(8,128)S(1)}, f32[3,32,768]{2,1,0:T(8,128)S(1)}) fusion(f32[3]{0:T(128)S(1)} %broadcast_divide_fusion, s32[3]{0:T(128)S(1)} %get-tuple-element.26, s32[32,768]{1,0:T(8,128)S(1)} %iota_multiply_fusion.1, pred[3]{0:T(512)(128)(4,1)S(1)} %broadcast_compare_fusion), kind=kLoop, calls=%fused_computation.54 | loop fusion | flops 663552 | bytes 688155 | tf_op jit(solution)/shard_map/cos | solution.py:49
  24.3 7.5 %multiply_subtract_fusion = (f32[3,48,32,768]{3,2,1,0:T(8,128)S(1)}, f32[3,48,32,768]{3,2,1,0:T(8,128)}) fusion(f32[3,32,768]{2,1,0:T(8,128)S(1)} %get-tuple-element.17, f32[3,48,768]{2,1,0:T(8,128)S(1)} %get-tuple-element.15, f32[3,32,768]{2,1,0:T(8,128)S(1)} %get-tuple-element.16, f32[3,48,768]{2,1,0:T(8,128)S(1)} %get-tuple-element.14), kind=kLoop, calls=%fused_computation.11 | loop fusion | flops 24772608 | bytes 29786112 | tf_op jit(solution)/shard_map/sub | solution.py:52
  31.8 14.3 %and_select_fusion.1 = (f32[3,1536,768]{2,1,0:T(8,128)}, f32[3,1536,768]{2,1,0:T(8,128)}) fusion(f32[3,48,32,768]{3,2,1,0:T(8,128)S(1)} %get-tuple-element.12, pred[3,768]{1,0:T(4,128)(4,1)S(1)} %iota_compare_fusion.2, pred[3,1536]{1,0:T(4,128)(4,1)S(1)} %iota_compare_fusion, f32[3,48,32,768]{3,2,1,0:T(8,128)} %get-tuple-element.13), kind=kLoop, calls=%fused_computation.9 | loop fusion | flops 10616832 | bytes 56630016 | tf_op jit(solution)/shard_map/jit(_where)/select_n | solution.py:60
  46.1 0.7 copy.48
  46.8 1.2 reshape.709
  48.0 20.4 %fusion.12 = f32[3,96,1536]{2,1,0:T(8,128)S(1)} fusion(f32[3,96,1536]{2,1,0:T(8,128)S(1)} %reshape.709, f32[3,1536,768]{2,1,0:T(8,128)} %get-tuple-element.19, f32[3,1536,768]{2,1,0:T(8,128)} %get-tuple-element.18, f32[3]{0:T(128)S(1)} %get-tuple-element.6), kind=kOutput, calls=%fused_computation.26 | convolution fusion | flops 8161247232 | bytes 31850508 | tf_op jit(solution)/shard_map/pqx,pxk->pqk/dot_general | solution.py:82
  68.4 1.4 copy.94
  69.8 2.9 copy.50
  72.8 4.3 %gather_fusion.1 = f32[768,3,192]{2,1,0:T(4,128)} fusion(f32[768,3,192]{2,1,0:T(4,128)S(1)} %copy.50, s32[1024]{0:T(1024)S(1)} %pad_clamp_fusion.1), kind=kCustom, calls=%fused_computation.clone | custom fusion | bytes 3542016 | tf_op jit(solution)/shard_map/jit(_take)/gather | solution.py:90
  77.1 4.2 %broadcast_select_fusion.1 = f32[768,3,192]{2,1,0:T(4,128)S(1)} fusion(f32[768,3,192]{2,1,0:T(4,128)} %gather_fusion.1, pred[768]{0:T(1024)(128)(4,1)S(1)} %compare_and_fusion.1), kind=kLoop, calls=%fused_computation.28 | loop fusion | flops 442368 | bytes 3539712 | tf_op jit(solution)/shard_map/jit(_take)/select_n | solution.py:90
  81.3 3.9 %copy.52 = f32[128,1,1,6,1,1,3,192]{7,5,6,4,3,2,1,0:T(1,128)} copy(f32[128,1,1,6,1,1,3,192]{7,6,3,0,5,4,2,1:T(4,128)S(1)} %bitcast.105) | data formatting | bytes 3538944 | tf_op jit(solution)/shard_map/reshape;transpose;transpose;reshape;reshape;reshape | solution.py:27
  85.2 10.7 %all-to-all-start.1 = ((f32[128,1,1,6,1,1,3,192]{7,5,6,4,3,2,1,0:T(1,128)}), f32[128,1,1,6,1,1,3,192]{7,5,6,4,3,2,1,0:T(1,128)S(1)}, u32[]{:S(2)}, u32[]{:S(2)}) async-start(f32[128,1,1,6,1,1,3,192]{7,5,6,4,3,2,1,0:T(1,128)} %copy.52), calls=%async_computation.1 | async-start | bytes 4718592 | tf_op jit(solution)/shard_map/all_to_all | solution.py:28
  96.0 0.6 gather_fusion
  97.1 0.9 add_divide_fusion
  98.0 31.1 %all-to-all-done.1 = f32[128,1,1,6,1,1,3,192]{7,5,6,4,3,2,1,0:T(1,128)S(1)} async-done(((f32[128,1,1,6,1,1,3,192]{7,5,6,4,3,2,1,0:T(1,128)}), f32[128,1,1,6,1,1,3,192]{7,5,6,4,3,2,1,0:T(1,128)S(1)}, u32[]{:S(2)}, u32[]{:S(2)}) %all-to-all-start.1) | async-done | bytes 1769504 | tf_op jit(solution)/shard_map/all_to_all | solution.py:28
  129.2 1.5 copy-done.1
  130.7 2.1 copy.93
  132.8 2.5 reshape_reshape_reshape_reshape.6
  135.4 2.7 broadcast_multiply_fusion.1
  138.1 17.1 %fusion.5 = f32[3,769,2,192]{1,3,2,0:T(8,128)} fusion(f32[3,384,769]{1,2,0:T(8,128)S(1)} %copy-done, f32[3,2,384,192]{3,1,0,2:T(2,128)S(1)} %broadcast_multiply_fusion.1), kind=kOutput, calls=%fused_computation.17 | convolution fusion | flops 4082171904 | bytes 8856576 | tf_op jit(solution)/shard_map/sjc,sejr->scer/dot_general | solution.py:110
  155.2 6.1 %reshape.715 = f32[3,769,2,2,48,2]{1,5,4,3,2,0:T(2,128)} reshape(f32[3,769,2,192]{1,3,2,0:T(8,128)} %fusion.5) | data formatting | bytes 7087104 | tf_op jit(solution)/shard_map/reshape | solution.py:111
  161.3 3.3 %fusion.10 = f32[3,769,2,48,2]{1,4,3,2,0:T(2,128)S(1)} fusion(f32[3,769,2,2,48,2]{1,5,4,3,2,0:T(2,128)} %reshape.715, pred[3,769]{1,0:T(4,128)(4,1)S(1)} %iota_compare_fusion.1), kind=kLoop, calls=%fused_computation.19 | loop fusion | flops 442944 | bytes 5317635 | tf_op jit(solution)/shard_map/jit(_where)/select_n | solution.py:112
  164.6 1.6 fusion.48
  166.5 4.0 %broadcast_multiply_fusion = f32[3,769,2,2,48,2]{1,5,4,3,2,0:T(2,128)} fusion(f32[3,769,2]{1,2,0:T(2,128)S(1)} %stack.22, f32[3,769,2,2,48]{1,4,3,2,0:T(8,128)S(1)} %broadcast_multiply_fusion.2), kind=kLoop, calls=%fused_computation.21 | loop fusion | flops 885888 | bytes 5333784 | tf_op jit(solution)/shard_map/mul | solution.py:123
  170.5 6.0 %mul.286 = f32[3,769,384]{1,2,0:T(8,128)} reshape(f32[3,769,2,2,48,2]{1,5,4,3,2,0:T(2,128)} %broadcast_multiply_fusion) | data formatting | bytes 7087104 | tf_op jit(solution)/shard_map/mul | solution.py:123
  176.5 9.3 %fusion.49 = f32[3,384,384]{2,1,0:T(8,128)S(1)} fusion(f32[3,769,384]{1,2,0:T(8,128)} %mul.286, f32[3,384,769]{1,2,0:T(8,128)} %param.14), kind=kOutput, calls=%fused_computation.122 | convolution fusion | flops 4082171904 | bytes 8856576 | tf_op jit(solution)/shard_map/sjc,scr->sjr/dot_general | solution.py:125
  185.8 3.3 %copy.58 = f32[3,384,2,192]{3,2,0,1:T(2,128)} copy(f32[3,384,2,192]{1,3,2,0:T(8,128)S(1)} %bitcast.117) | data formatting | bytes 3538944 | tf_op jit(solution)/shard_map/reshape | solution.py:126
  189.1 3.3 %reshape_reshape_reshape_reshape.7 = f32[1,1,6,32,1,4,3,192]{7,2,6,5,3,4,1,0:T(8,128)S(1)} reshape(f32[3,2,384,192]{3,1,0,2:T(2,128)} %bitcast.110) | data formatting | bytes 3538944 | tf_op jit(solution)/shard_map/reshape;reshape;reshape;reshape | solution.py:13
  192.4 3.9 %copy.59 = f32[128,1,1,6,1,1,3,192]{7,5,6,4,3,2,1,0:T(1,128)} copy(f32[128,1,1,6,1,1,3,192]{7,3,6,0,5,4,2,1:T(8,128)S(1)} %bitcast.107) | data formatting | bytes 3538944 | tf_op jit(solution)/shard_map/reshape | solution.py:27
  196.3 3.8 %all-to-all-start.2 = ((f32[128,1,1,6,1,1,3,192]{7,5,6,4,3,2,1,0:T(1,128)}), f32[128,1,1,6,1,1,3,192]{7,5,6,4,3,2,1,0:T(1,128)S(1)}, u32[]{:S(2)}, u32[]{:S(2)}) async-start(f32[128,1,1,6,1,1,3,192]{7,5,6,4,3,2,1,0:T(1,128)} %copy.59), calls=%async_computation.2 | async-start | bytes 4718592 | tf_op jit(solution)/shard_map/all_to_all | solution.py:28
  200.3 3.4 %scatter_custom_fusion.1 = s32[768]{0:T(1024)S(1)} fusion(s32[768]{0:T(1024)S(1)} %fusion.39, s32[768]{0:T(1024)S(1)} %iota.109, s32[]{:T(128)} %constant.72.clone.1), kind=kCustom, calls=%fused_computation.102 | custom fusion | bytes 3076 | tf_op jit(solution)/shard_map/scatter | solution.py:135
  203.7 29.8 %all-to-all-done.2 = f32[128,1,1,6,1,1,3,192]{7,5,6,4,3,2,1,0:T(1,128)S(1)} async-done(((f32[128,1,1,6,1,1,3,192]{7,5,6,4,3,2,1,0:T(1,128)}), f32[128,1,1,6,1,1,3,192]{7,5,6,4,3,2,1,0:T(1,128)S(1)}, u32[]{:S(2)}, u32[]{:S(2)}) %all-to-all-start.2) | async-done | bytes 1769504 | tf_op jit(solution)/shard_map/all_to_all | solution.py:28
  233.6 0.5 copy.92
  234.0 1.9 copy.70
  236.0 4.5 %gather_fusion.2 = f32[768,3,192]{2,1,0:T(4,128)} fusion(f32[768,3,192]{2,1,0:T(4,128)S(1)} %bitcast.103, s32[1024]{0:T(1024)S(1)} %pad_clamp_fusion), kind=kCustom, calls=%fused_computation.1.clone | custom fusion | bytes 3542016 | tf_op jit(solution)/shard_map/jit(_take)/gather | solution.py:137
  240.4 4.2 %broadcast_select_fusion = f32[768,3,192]{2,1,0:T(4,128)S(1)} fusion(f32[768,3,192]{2,1,0:T(4,128)} %gather_fusion.2, pred[768]{0:T(1024)(128)(4,1)S(1)} %compare_and_fusion), kind=kLoop, calls=%fused_computation.27 | loop fusion | flops 442368 | bytes 3539712 | tf_op jit(solution)/shard_map/jit(_take)/select_n | solution.py:137
  244.7 2.3 copy.62
  247.0 1.7 copy.75
  248.7 30.9 %fusion = f32[3,96,1536]{2,1,0:T(8,128)S(1)} fusion(f32[3,1536,768]{2,1,0:T(8,128)} %get-tuple-element.19, f32[3,1536,768]{2,1,0:T(8,128)} %get-tuple-element.18, f32[3,96,1536]{2,1,0:T(8,128)S(1)} %bitcast.102, f32[1536]{0:T(1024)S(1)} %fusion.38), kind=kOutput, calls=%fused_computation.6 | convolution fusion | flops 8161247232 | bytes 31856640 | tf_op jit(solution)/shard_map/pqk,pxk->pqx/dot_general | solution.py:143
  279.6 1.1 reshape.724
  280.6 0.6 copy.95
  281.2 25.1 %all_to_all.46 = f32[3,16,3,2,1536]{4,3,0,2,1:T(2,128)S(1)} all-to-all(f32[3,16,3,2,1536]{4,3,0,2,1:T(2,128)S(1)} %bitcast.115), channel_id=1, replica_groups=mesh['band'=32,'lev'=4] {'lev'}, dimensions={1} | all-to-all | bytes 3538944 | tf_op jit(solution)/shard_map/all_to_all | solution.py:150
  306.4 2.1 copy.65
  (57 shorter events, 1.7 us)
Async XLA Ops:
  0.0 10.3 %copy-start.8 = (s32[12]{0:T(128)S(1)}, s32[12]{0:T(128)}, u32[]{:S(2)}) copy-start(s32[12]{0:T(128)} %param.11) | copy-start | bytes 148
  4.3 6.2 %copy-start.7 = (s32[384]{0:T(512)S(1)}, s32[384]{0:T(512)}, u32[]{:S(2)}) copy-start(s32[384]{0:T(512)} %param.13) | copy-start | bytes 4612
  4.3 41.8 %all-to-all-start = ((f32[3,4,12,2,1536]{4,3,1,0,2:T(2,128)}), f32[3,4,12,2,1536]{4,3,1,0,2:T(2,128)S(1)}, u32[]{:S(2)}, u32[]{:S(2)}) async-start(f32[3,4,12,2,1536]{4,3,1,0,2:T(2,128)} %copy_add_fusion), calls=%async_computation | async-start | bytes 3538944 | tf_op jit(solution)/shard_map/all_to_all | solution.py:76
  13.8 0.7 copy-start.3
  85.2 11.4 %copy-start.6 = (f32[3,16]{1,0:T(4,128)S(1)}, f32[3,16]{1,0:T(4,128)}, u32[]{:S(2)}) copy-start(f32[3,16]{1,0:T(4,128)} %param.15) | copy-start | bytes 580
  85.2 44.0 %all-to-all-start.1 = ((f32[128,1,1,6,1,1,3,192]{7,5,6,4,3,2,1,0:T(1,128)}), f32[128,1,1,6,1,1,3,192]{7,5,6,4,3,2,1,0:T(1,128)S(1)}, u32[]{:S(2)}, u32[]{:S(2)}) async-start(f32[128,1,1,6,1,1,3,192]{7,5,6,4,3,2,1,0:T(1,128)} %copy.52), calls=%async_computation.1 | async-start | bytes 4718592 | tf_op jit(solution)/shard_map/all_to_all | solution.py:28
  129.2 1.5 copy-start.1
  132.8 2.6 copy-start.5
  135.4 2.7 copy-start
  164.6 1.6 copy-start.2
  196.3 3.8 %copy-start.4 = (s32[384,2]{1,0:T(8,128)S(1)}, s32[384,2]{1,0:T(8,128)}, u32[]{:S(2)}) copy-start(s32[384,2]{1,0:T(8,128)} %copy-done.3) | copy-start | bytes 9220
  196.3 37.2 %all-to-all-start.2 = ((f32[128,1,1,6,1,1,3,192]{7,5,6,4,3,2,1,0:T(1,128)}), f32[128,1,1,6,1,1,3,192]{7,5,6,4,3,2,1,0:T(1,128)S(1)}, u32[]{:S(2)}, u32[]{:S(2)}) async-start(f32[128,1,1,6,1,1,3,192]{7,5,6,4,3,2,1,0:T(1,128)} %copy.59), calls=%async_computation.2 | async-start | bytes 4718592 | tf_op jit(solution)/shard_map/all_to_all | solution.py:28
where the time goes:
time: 312 us; the launch traced here: 309 us
  matrix products  77.7 us (25%)
  local copies, waits for them, and re-layouts  67.6 us (22%)
  waiting for transfers between devices  61 us (20%)
  other arithmetic  56.2 us (18%)
  blocking collectives  25.1 us (8%)
  starting transfers between devices  20.5 us (7%)
    all_to_all x2, waiting for transfers between devices, one_exchange(): lax.all_to_all(blocks, axis, split_axis=0, concat_axis=0, tiled=True)  61 us
    dot_general x1, matrix products, body(): jnp.einsum('pqk,pxk->pqx', spectral_rows * doubling[None, None, :], table...  30.9 us
    all_to_all x1, blocking collectives, body(): lax.all_to_all(grid_rows, 'lev', split_axis=1, concat_axis=2, tiled=True)  25.1 us
    dot_general x1, matrix products, body(): jnp.einsum('pqx,pxk->pqk', pair_rows, tables, precision=lax.Precision.HIG...  20.4 us
    dot_general x1, matrix products, body(): jnp.einsum('sjc,sejr->scer', legendre, weighted, precision=lax.Precision....  17.1 us
    all_to_all x2, starting transfers between devices, one_exchange(): lax.all_to_all(blocks, axis, split_axis=0, concat_axis=0, tiled=True)  14.5 us
    select_n x1, other arithmetic, dft_tables(): cosines = jnp.where(live, full_cos, 0.0)  14.3 us
    dot_general x1, matrix products, body(): jnp.einsum('sjc,scr->sjr', legendre, spread, precision=lax.Precision.HIGH...  9.3 us
  transfers between devices with their start and end apart: 3, of which 2 were waited for; matrix products, arithmetic and copies ran while one was open for 13% of the time, Pallas kernels for 0%

commit v1 on v0

v1 whole, which is shorter than its diff:
```python
import functools
import math

import jax
import jax.numpy as jnp
from jax import lax
from jax.experimental import pallas as pl
from jax.experimental.pallas import tpu as pltpu
from jax.sharding import PartitionSpec as P

MESH = pl.DeviceIdType.MESH
F32 = jnp.float32
BF16 = jnp.bfloat16
SIN_COEFS = [(-1) ** k * math.pi ** (2 * k + 1) / math.factorial(2 * k + 1) for k in range(7)]
COS_COEFS = [(-1) ** k * math.pi ** (2 * k) / math.factorial(2 * k) for k in range(8)]


def half_turn_pair(half):
    square = half * half
    sine = jnp.full_like(square, SIN_COEFS[-1])
    for coef in SIN_COEFS[-2::-1]:
        sine = sine * square + coef
    cosine = jnp.full_like(square, COS_COEFS[-1])
    for coef in COS_COEFS[-2::-1]:
        cosine = cosine * square + coef
    return cosine, sine * half


def turn_pair(orders, doubled, count):
    period = 2.0 * count
    product = orders * doubled
    rest = product - jnp.round(product / period) * period
    cosine, sine = half_turn_pair(rest / period)
    return 1.0 - 2.0 * sine * sine, 2.0 * sine * cosine


def split(value):
    high = value.astype(BF16)
    return high, (value - high.astype(F32)).astype(BF16)


def wide_dot(left, right, contract):
    return lax.dot_general(left, right, (contract, ((), ())), preferred_element_type=F32)


def phase_rows(orders, count):
    row = lax.broadcasted_iota(jnp.int32, (8, orders.shape[1]), 0)
    fine = 2 * row + 1
    step = jnp.where(row < 4, jnp.left_shift(16, jnp.minimum(row, 4)), (row - 4) * 512 + 256)
    step = jnp.where(row == 7, 1535, step)
    wide = jnp.broadcast_to(orders, (8, orders.shape[1]))
    fine_pair = turn_pair(wide, fine.astype(F32), count)
    step_pair = turn_pair(wide, step.astype(F32), count)
    return fine_pair, step_pair


def fill_tables(fine_pair, step_pair, cos_hi, cos_lo, sin_hi, sin_lo):
    cosine, sine = fine_pair
    step_cos, step_sin = step_pair
    for level in range(4):
        turn_cos = step_cos[level : level + 1]
        turn_sin = step_sin[level : level + 1]
        next_cos = cosine * turn_cos - sine * turn_sin
        next_sin = sine * turn_cos + cosine * turn_sin
        cosine = jnp.concatenate([cosine, next_cos], axis=0)
        sine = jnp.concatenate([sine, next_sin], axis=0)
    high, low = split(cosine)
    cos_hi[...] = high
    cos_lo[...] = low
    high, low = split(sine)
    sin_hi[...] = high
    sin_lo[...] = low


def reversed_lanes(value):
    index = 127 - lax.broadcasted_iota(jnp.int32, value.shape, 1)
    return jnp.take_along_axis(value, index, axis=1)


def forward_kernel(points, weights, orders_ref, field, increment, out, rows, spectra, cos_hi, cos_lo, sin_hi, sin_lo):
    pair = pl.program_id(0)
    for f in range(3):
        for l in range(4):
            at = 8 * f + 2 * l
            rows[at : at + 2, :] = field[f, l, 0] + increment[f, l, 0]
    count = points[0, pair].astype(F32)
    band = lax.axis_index("band")
    weight = weights[band * 12 + pair]
    orders = orders_ref[...]
    fine_pair, step_pair = phase_rows(orders, count)
    fill_tables(fine_pair, step_pair, cos_hi, cos_lo, sin_hi, sin_lo)
    step_cos, step_sin = step_pair
    value = rows[...]
    place = lax.broadcasted_iota(jnp.int32, value.shape, 1).astype(F32)
    value = jnp.where(place < count, value, 0.0)
    even, odd = [], []
    for block in range(6):
        low = reversed_lanes(value[:, 256 * block : 256 * block + 128])
        high = value[:, 256 * block + 128 : 256 * block + 256]
        even.append(high + low)
        odd.append(high - low)

    def folded(parts):
        return jnp.concatenate(
            [parts[3 + g] + parts[2 - g] for g in range(3)] + [parts[3 + g] - parts[2 - g] for g in range(3)],
            axis=0,
        )

    def product(parts, table_hi, table_lo):
        high, low = split(folded(parts))
        both = jnp.concatenate([high, low], axis=1)
        twice = jnp.concatenate([table_hi[...], table_hi[...]], axis=0)
        contract = ((1,), (0,))
        return wide_dot(both, twice, contract) + wide_dot(high, table_lo[...], contract)

    by_cos = product(even, cos_hi, cos_lo)
    by_sin = product(odd, sin_hi, sin_lo)
    real = jnp.zeros((24, 768), F32)
    imag = jnp.zeros((24, 768), F32)
    for g in range(3):
        plus = slice(24 * g, 24 * g + 24)
        minus = slice(72 + 24 * g, 96 + 24 * g)
        turn_cos = step_cos[4 + g : 5 + g]
        turn_sin = step_sin[4 + g : 5 + g]
        real = real + turn_cos * by_cos[plus] - turn_sin * by_sin[minus]
        imag = imag - turn_sin * by_cos[minus] - turn_cos * by_sin[plus]
    live = (2.0 * orders + 1.0 <= count).astype(F32) * (weight / count)
    centre_cos = step_cos[7:8] * live
    centre_sin = step_sin[7:8] * live
    both = (real * centre_cos + imag * centre_sin, imag * centre_cos - real * centre_sin)
    for t in range(6):
        for r in range(2):
            at = (t // 3) * 1728 + (t % 3) * 48 + r * 24
            spectra[pl.ds(at + pair * 144, 24), :] = both[r][:, 128 * t : 128 * t + 128]

    @pl.when(pair == 11)
    def _():
        for c in range(27):
            out[c] = spectra[128 * c : 128 * c + 128, :].T


def inverse_kernel(points, orders_ref, spectra_in, out, rows, spectra, cos_hi, cos_lo, sin_hi, sin_lo):
    pair = pl.program_id(0)

    @pl.when(pair == 0)
    def _():
        for c in range(27):
            spectra[128 * c : 128 * c + 128, :] = spectra_in[c].T

    count = points[0, pair].astype(F32)
    orders = orders_ref[...]
    fine_pair, step_pair = phase_rows(orders, count)
    fill_tables(fine_pair, step_pair, cos_hi, cos_lo, sin_hi, sin_lo)
    step_cos, step_sin = step_pair

    def part(r):
        return jnp.concatenate(
            [
                spectra[pl.ds((t // 3) * 1728 + (t % 3) * 48 + r * 24 + pair * 144, 24), :]
                for t in range(6)
            ],
            axis=1,
        )

    in_real, in_imag = part(0), part(1)
    live = 2.0 * orders + 1.0 <= count
    doubling = jnp.where(live, jnp.where(orders < 0.5, 1.0, 2.0), 0.0)
    centre_cos = step_cos[7:8] * doubling
    centre_sin = step_sin[7:8] * doubling
    real = in_real * centre_cos - in_imag * centre_sin
    imag = in_real * centre_sin + in_imag * centre_cos

    def turned(first, second):
        return jnp.concatenate(
            [first * step_cos[4 + g : 5 + g] for g in range(3)]
            + [second * step_sin[4 + g : 5 + g] for g in range(3)],
            axis=0,
        )

    def product(first, second, table_hi, table_lo):
        high, low = split(turned(first, second))
        contract = ((1,), (1,))
        both = wide_dot(high, jnp.concatenate([table_hi[...], table_lo[...]], axis=0), contract)
        return both[:, :128] + both[:, 128:] + wide_dot(low, table_hi[...], contract)

    by_cos = product(real, imag, cos_hi, cos_lo)
    by_sin = product(imag, real, sin_hi, sin_lo)
    place = lax.broadcasted_iota(jnp.int32, (24, 128), 1).astype(F32)

    def put(block, value):
        rows[:, 128 * block : 128 * block + 128] = jnp.where(place + 128.0 * block < count, value, 0.0)

    for g in range(3):
        c1, c2 = by_cos[24 * g : 24 * g + 24], by_cos[72 + 24 * g : 96 + 24 * g]
        s1, s2 = by_sin[24 * g : 24 * g + 24], by_sin[72 + 24 * g : 96 + 24 * g]
        minus, plus = c1 - c2, c1 + c2
        total, differ = s1 + s2, s1 - s2
        put(2 * (3 + g) + 1, minus - total)
        put(2 * (3 + g), reversed_lanes(minus + total))
        put(2 * (2 - g) + 1, plus - differ)
        put(2 * (2 - g), reversed_lanes(plus + differ))
    for f in range(3):
        for l in range(4):
            at = 8 * f + 2 * l
            out[f, l, 0] = rows[at : at + 2, :]


def block_swap(parts):
    lane = lax.broadcasted_iota(jnp.int32, parts[0].shape, 1)
    far = lane < 64
    near = (lane // 32) % 2 == 0
    a, b, c, d = parts
    a, c = jnp.where(far, a, pltpu.roll(c, 64, 1)), jnp.where(far, pltpu.roll(a, 64, 1), c)
    b, d = jnp.where(far, b, pltpu.roll(d, 64, 1)), jnp.where(far, pltpu.roll(b, 64, 1), d)
    a, b = jnp.where(near, a, pltpu.roll(b, 32, 1)), jnp.where(near, pltpu.roll(a, 96, 1), b)
    c, d = jnp.where(near, c, pltpu.roll(d, 32, 1)), jnp.where(near, pltpu.roll(c, 96, 1), d)
    return a, b, c, d


def hemispheres(value):
    row = lax.broadcasted_iota(jnp.int32, value.shape, 0)
    first = row % 2 == 0
    n = value.shape[0]
    other = jnp.where(first, pltpu.roll(value, n - 1, 0), pltpu.roll(value, 1, 0))
    return other + jnp.where(first, value, -value)


def legendre_kernel(lowers, rates, legendre, arrived, out, flat, left, back, tiled, table_hi, table_lo):
    slot = pl.program_id(0)
    me = lax.axis_index("band") * 4 + lax.axis_index("lev")

    @pl.when(slot == 0)
    def _():
        for c in range(27):
            flat[128 * c : 128 * c + 128, :] = arrived[c].T

    def at(member, i, r, f):
        return member * 1728 + i * 144 + r * 24 + f * 8

    for c in range(6):
        tiled[c] = legendre[0, :, 128 * c : 128 * c + 128]
    first_lane = lax.broadcasted_iota(jnp.int32, (384, 128), 1) == 0
    tiled[6] = jnp.where(first_lane, legendre[0, :, 768:769], 0.0)
    for i in range(12):
        for c in range(7):
            high, low = split(tiled[c, pl.ds(i, 32, stride=12), :])
            table_hi[32 * i : 32 * i + 32, 128 * c : 128 * c + 128] = high
            table_lo[32 * i : 32 * i + 32, 128 * c : 128 * c + 128] = low
    for member in range(2):
        for r in range(2):
            for f in range(3):
                for g in range(3):
                    parts = [flat[pl.ds(at(member, 4 * g + k, r, f) + slot * 48, 8), :] for k in range(4)]
                    for z, value in enumerate(block_swap(parts)):
                        row = ((member * 2 + r) * 4 + z) * 24 + f * 8
                        left[row : row + 8, 128 * g : 128 * g + 128] = hemispheres(value)
    lower = lowers[slot, me].astype(F32)
    column = lax.broadcasted_iota(jnp.int32, (8, 896), 1).astype(F32)
    row = lax.broadcasted_iota(jnp.int32, (8, 896), 0)
    second = column >= 768.0 - lower
    degree = jnp.where(second, column - 1.0, lower + column)
    order = jnp.where(second, 767.0 - lower, lower)
    gap = degree - order
    odd = gap - 2.0 * jnp.floor(gap * 0.5)
    wanted = jnp.where(row % 2 == 0, 1.0 - odd, odd)
    ratio = degree * (degree + 1.0) / float(767 * 768)
    square = ratio * ratio
    for member in range(2):
        kept = jnp.where(second, 1.0, 0.0) if member else jnp.where(second, 0.0, 1.0)
        kept = kept * wanted
        for r in range(2):
            top = (member * 2 + r) * 96
            value = left[top : top + 96, :]
            high, low = split(value)
            contract = ((1,), (0,))
            coef = wide_dot(high, table_hi[...], contract) + wide_dot(high, table_lo[...], contract)
            coef = coef + wide_dot(low, table_hi[...], contract)
            scale = jnp.concatenate([kept / (1.0 + rates[8 * k : 8 * k + 8, :] * square) for k in range(12)], axis=0)
            damped = coef * scale
            high, low = split(damped)
            contract = ((1,), (1,))
            given = wide_dot(high, table_hi[...], contract) + wide_dot(high, table_lo[...], contract)
            given = given + wide_dot(low, table_hi[...], contract)
            back[top : top + 96, :] = given
    for member in range(2):
        for r in range(2):
            for f in range(3):
                for g in range(3):
                    parts = []
                    for z in range(4):
                        row = ((member * 2 + r) * 4 + z) * 24 + f * 8
                        parts.append(hemispheres(back[row : row + 8, 128 * g : 128 * g + 128]))
                    for k, value in enumerate(block_swap(parts)):
                        flat[pl.ds(at(member, 4 * g + k, r, f) + slot * 48, 8), :] = value

    @pl.when(slot == 2)
    def _():
        for c in range(27):
            out[c] = flat[128 * c : 128 * c + 128, :].T


def exchange_kernel(forward, source, out, held, got, send_sem, recv_sem, local_sem):
    band, lev = lax.axis_index("band"), lax.axis_index("lev")
    me = band * 4 + lev
    barrier = pltpu.get_barrier_semaphore()

    def peer(k):
        t = lax.rem(me + k, 128)
        return t, t // 4, lax.rem(t, 4)

    def greet(k, carry):
        _, b, z = peer(k)
        pl.semaphore_signal(barrier, inc=1, device_id=(b, z), device_id_type=MESH)
        return carry

    load = pltpu.make_async_copy(source, held, local_sem)
    load.start()
    lax.fori_loop(1, 128, greet, 0)
    mine_device, mine_grid = me, lev * 32 + band
    load.wait()
    here = (mine_device, mine_grid) if forward else (mine_grid, mine_device)
    got[:, pl.ds(here[1], 1), :] = held[:, pl.ds(here[0], 1), :]
    pl.semaphore_wait(barrier, 127)

    def copy(k):
        t, b, z = peer(k)
        grid = z * 32 + b
        row, place = (t, mine_grid) if forward else (grid, mine_device)
        return pltpu.make_async_remote_copy(
            src_ref=held.at[:, pl.ds(row, 1), :],
            dst_ref=got.at[:, pl.ds(place, 1), :],
            send_sem=send_sem,
            recv_sem=recv_sem,
            device_id=(b, z),
            device_id_type=MESH,
        )

    def begin(k, carry):
        copy(k).start()
        return carry

    lax.fori_loop(1, 128, begin, 0)
    everything = pltpu.make_async_remote_copy(
        src_ref=held.at[:, pl.ds(0, 127), :],
        dst_ref=got.at[:, pl.ds(0, 127), :],
        send_sem=send_sem,
        recv_sem=recv_sem,
        device_id=(band, lev),
        device_id_type=MESH,
    )
    everything.wait()
    store = pltpu.make_async_copy(got, out, local_sem)
    store.start()
    store.wait()


BLOCKS = jax.ShapeDtypeStruct((27, 128, 128), F32)
ANYWHERE = pl.BlockSpec(memory_space=pl.ANY)
SCALARS = pl.BlockSpec(memory_space=pltpu.SMEM)


def exchange(value, forward):
    return pl.pallas_call(
        functools.partial(exchange_kernel, forward),
        out_shape=BLOCKS,
        in_specs=[ANYWHERE],
        out_specs=ANYWHERE,
        scratch_shapes=[
            pltpu.VMEM((27, 128, 128), F32),
            pltpu.VMEM((27, 128, 128), F32),
            pltpu.SemaphoreType.DMA,
            pltpu.SemaphoreType.DMA,
            pltpu.SemaphoreType.DMA,
        ],
        compiler_params=pltpu.CompilerParams(collective_id=0 if forward else 1, has_side_effects=True),
        name="exchange_out" if forward else "exchange_back",
    )(value)


TABLES = [pltpu.VMEM((128, 768), BF16) for _ in range(4)]
GRID_BLOCK = pl.BlockSpec((3, 4, 1, 2, 1536), lambda i: (0, 0, i, 0, 0))
WHOLE = pl.BlockSpec((27, 128, 128), lambda i: (0, 0, 0))


def forward_part(points, weights, orders, field_grid, increment):
    return pl.pallas_call(
        forward_kernel,
        grid=(12,),
        out_shape=BLOCKS,
        in_specs=[SCALARS, SCALARS, pl.BlockSpec((1, 768), lambda i: (0, 0)), GRID_BLOCK, GRID_BLOCK],
        out_specs=WHOLE,
        scratch_shapes=[pltpu.VMEM((24, 1536), F32), pltpu.VMEM((3456, 128), F32)] + TABLES,
        name="forward",
    )(points, weights, orders, field_grid, increment)


def inverse_part(points, orders, spectra):
    return pl.pallas_call(
        inverse_kernel,
        grid=(12,),
        out_shape=jax.ShapeDtypeStruct((3, 4, 12, 2, 1536), F32),
        in_specs=[SCALARS, pl.BlockSpec((1, 768), lambda i: (0, 0)), WHOLE],
        out_specs=GRID_BLOCK,
        scratch_shapes=[pltpu.VMEM((24, 1536), F32), pltpu.VMEM((3456, 128), F32)] + TABLES,
        name="inverse",
    )(points, orders, spectra)


def legendre_part(lowers, rates, legendre, arrived):
    return pl.pallas_call(
        legendre_kernel,
        grid=(3,),
        out_shape=BLOCKS,
        in_specs=[
            SCALARS,
            pl.BlockSpec((96, 1), lambda i: (0, 0)),
            pl.BlockSpec((1, 384, 769), lambda i: (i, 0, 0)),
            WHOLE,
        ],
        out_specs=WHOLE,
        scratch_shapes=[
            pltpu.VMEM((3456, 128), F32),
            pltpu.VMEM((384, 384), F32),
            pltpu.VMEM((384, 384), F32),
            pltpu.VMEM((7, 384, 128), F32),
            pltpu.VMEM((384, 896), BF16),
            pltpu.VMEM((384, 896), BF16),
        ],
        name="legendre",
    )(lowers, rates, legendre, arrived)


def body(field_grid, increment, points, weights, pair_slot, legendre, strength):
    slots = 3 * lax.broadcasted_iota(jnp.int32, (3, 128, 1), 1) + lax.broadcasted_iota(jnp.int32, (3, 128, 1), 0)
    waves = lax.broadcasted_iota(jnp.int32, (1, 1, 384), 2)
    lowers = jnp.sum(jnp.where(pair_slot[None, None, :] == slots, waves, 0), axis=2)
    orders = jnp.concatenate([lowers.reshape(1, 384), 767 - lowers.reshape(1, 384)], axis=1).astype(F32)
    rates = strength.reshape(3, 4, 4).transpose(1, 0, 2)
    rates = jnp.broadcast_to(rates[..., None], (4, 3, 4, 2)).reshape(96, 1)
    counts = points.reshape(1, 12)
    sent = forward_part(counts, weights, orders, field_grid, increment)
    arrived = exchange(sent, True)
    given = legendre_part(lowers, rates, legendre, arrived)
    home = exchange(given, False)
    return inverse_part(counts, orders, home)


def solution(mesh):
    return jax.shard_map(
        body,
        mesh=mesh,
        in_specs=(
            P(None, "lev", "band", None, None),
            P(None, "lev", "band", None, None),
            P("band"),
            P(),
            P(),
            P(("band", "lev"), None, None),
            P(),
        ),
        out_specs=P(None, "lev", "band", None, None),
        check_vma=False,
    )
```

time: 312 us -> 126 us (0.40); the launches traced: 309 us -> 126 us
  Pallas kernels: 0 us -> 118 us
  matrix products: 77.7 us -> 0 us
  waiting for transfers between devices: 61 us -> 0 us
  local copies, waits for them, and re-layouts: 67.6 us -> 6.92 us
  other arithmetic: 56.2 us -> 1.52 us
  blocking collectives: 25.1 us -> 0 us
  starting transfers between devices: 20.5 us -> 0 us
    pallas_call x0 -> x5, Pallas kernels: none -> 118 us  [the longest x2 74.4 us: exchange(): pl.pallas_call(functools.partial(exchange_kernel, forward), out_shape=BLO...]
    dot_general x4 -> x0, matrix products: 77.7 us -> none  [the longest x1 30.9 us: body(): jnp.einsum('pqk,pxk->pqx', spectral_rows * doubling[None, None, :], table...]
    all_to_all x3 -> x0, waiting for transfers between devices: 61 us -> none  [the longest x2 61 us: one_exchange(): lax.all_to_all(blocks, axis, split_axis=0, concat_axis=0, tiled=True)]
    select_n x12 -> x0, other arithmetic: 26.2 us -> none  [the longest x1 14.3 us: dft_tables(): cosines = jnp.where(live, full_cos, 0.0)]
    all_to_all x1 -> x0, blocking collectives: 25.1 us -> none  [body(): lax.all_to_all(grid_rows, 'lev', split_axis=1, concat_axis=2, tiled=True)]
    reshape x13 -> x2, local copies, waits for them, and re-layouts: 25.1 us -> 1.47 us  [the longest x1 0.76 us: body(): rates = strength.reshape(3, 4, 4).transpose(1, 0, 2)]
    all_to_all x3 -> x0, starting transfers between devices: 20.5 us -> none  [the longest x2 14.5 us: one_exchange(): lax.all_to_all(blocks, axis, split_axis=0, concat_axis=0, tiled=True)]
    another operation x8 -> x0, local copies, waits for them, and re-layouts: 11.9 us -> none  [the longest x1 3.93 us: one_exchange(): blocks = blocks.reshape(-1, *inside)]
  transfers between devices with their start and end apart: 3 -> 0, of which waited for: 2 -> 0; matrix products, arithmetic and copies ran while one was open for 13% -> 0% of each run, Pallas kernels for 0% -> 0%
where the time goes in v1:
time: 126 us
  Pallas kernels  118 us (94%)
  local copies, waits for them, and re-layouts  6.92 us (5%)
  other arithmetic  1.52 us (1%)
    pallas_call x2, Pallas kernels, exchange(): pl.pallas_call(functools.partial(exchange_kernel, forward), out_shape=BLO...  74.4 us
    pallas_call x1, Pallas kernels, legendre_part(): pl.pallas_call(legendre_kernel, grid=(3,), out_shape=BLOCKS, in_specs=[SC...  19.7 us
    pallas_call x1, Pallas kernels, forward_part(): pl.pallas_call(forward_kernel, grid=(12,), out_shape=BLOCKS, in_specs=[SC...  12.1 us
    pallas_call x1, Pallas kernels, inverse_part(): pl.pallas_call(inverse_kernel, grid=(12,), out_shape=jax.ShapeDtypeStruct...  11.3 us
    unnamed x3, local copies, waits for them, and re-layouts  5.36 us

profile of v1, /device:TPU:1, one launch (start us, length us, event | category | flops | bytes accessed | tf_op | source)
XLA Modules:
  0.0 126.0 jit_solution(17229373999581106132)
XLA Ops:
  0.0 0.9 select_reduce_fusion.lowers
  0.9 0.0 copy-start
  1.0 0.6 add_convert_fusion.orders_ref
  1.5 0.8 reshape.69
  2.3 0.1 broadcast_in_dim.21
  2.4 0.7 reshape.71.rates
  3.1 12.1 %forward.1.source = f32[27,128,128]{2,1,0:T(8,128)} custom-call(s32[1,12]{1,0:T(1,128)} %bitcast.13, f32[384]{0:T(512)} %weights.1, f32[1,768]{1,0:T(1,128)} %add_convert_fusion.orders_ref, f32[3,4,12,2,1536]{4,3,2,1,0:T(2,128)} %field.1, f32[3,4,12,2,1536]{4,3,2,1,0:T(2,128)} %increment.1), custom_call_target="tpu_custom_call" | custom-call | tf_op jit(solution)/shard_map/forward/pallas_call | solution.py:386
  15.2 0.0 copy-done
  15.2 40.1 %exchange_out.1.arrived = f32[27,128,128]{2,1,0:T(8,128)} custom-call(f32[27,128,128]{2,1,0:T(8,128)} %forward.1.source), custom_call_target="tpu_custom_call" | custom-call | tf_op jit(solution)/shard_map/exchange_out/pallas_call | solution.py:363
  55.4 5.4 %copy.16.legendre = f32[3,384,769]{2,1,0:T(8,128)} copy(f32[3,384,769]{1,2,0:T(8,128)} %param.12) | data formatting | bytes 7087104 | tf_op args[5]
  60.7 19.7 %legendre.2.source = f32[27,128,128]{2,1,0:T(8,128)} custom-call(s32[3,128]{1,0:T(4,128)} %copy-done, f32[96,1]{1,0:T(8,128)} %reshape.71.rates, f32[3,384,769]{2,1,0:T(8,128)} %copy.16.legendre, f32[27,128,128]{2,1,0:T(8,128)} %exchange_out.1.arrived), custom_call_target="tpu_custom_call" | custom-call | tf_op jit(solution)/shard_map/legendre/pallas_call | solution.py:410
  80.4 34.2 %exchange_back.1.spectra_in = f32[27,128,128]{2,1,0:T(8,128)} custom-call(f32[27,128,128]{2,1,0:T(8,128)} %legendre.2.source), custom_call_target="tpu_custom_call" | custom-call | tf_op jit(solution)/shard_map/exchange_back/pallas_call | solution.py:363
  114.7 11.3 %inverse.1 = f32[3,4,12,2,1536]{4,3,2,1,0:T(2,128)} custom-call(s32[1,12]{1,0:T(1,128)} %bitcast.14, f32[1,768]{1,0:T(1,128)} %add_convert_fusion.orders_ref, f32[27,128,128]{2,1,0:T(8,128)} %exchange_back.1.spectra_in), custom_call_target="tpu_custom_call" | custom-call | tf_op jit(solution)/shard_map/inverse/pallas_call | solution.py:398
  (5 shorter events, 0.0 us)
Async XLA Ops:
  0.9 14.3 %copy-start = (s32[3,128]{1,0:T(4,128)}, s32[3,128]{1,0:T(4,128)S(1)}, u32[]{:S(2)}) copy-start(s32[3,128]{1,0:T(4,128)S(1)} %select_reduce_fusion.lowers) | copy-start | bytes 4612

commit v2 on v1

v2 whole, which is shorter than its diff:
```python
import math

import jax
import jax.numpy as jnp
from jax import lax
from jax.experimental import pallas as pl
from jax.experimental.pallas import tpu as pltpu
from jax.sharding import PartitionSpec as P

MESH = pl.DeviceIdType.MESH
F32 = jnp.float32
BF16 = jnp.bfloat16
SIN_COEFS = [(-1) ** k * math.pi ** (2 * k + 1) / math.factorial(2 * k + 1) for k in range(7)]
COS_COEFS = [(-1) ** k * math.pi ** (2 * k) / math.factorial(2 * k) for k in range(8)]


def half_turn_pair(half):
    square = half * half
    sine = jnp.full_like(square, SIN_COEFS[-1])
    for coef in SIN_COEFS[-2::-1]:
        sine = sine * square + coef
    cosine = jnp.full_like(square, COS_COEFS[-1])
    for coef in COS_COEFS[-2::-1]:
        cosine = cosine * square + coef
    return cosine, sine * half


def turn_pair(orders, doubled, count):
    period = 2.0 * count
    product = orders * doubled
    rest = product - jnp.round(product / period) * period
    cosine, sine = half_turn_pair(rest / period)
    return 1.0 - 2.0 * sine * sine, 2.0 * sine * cosine


def split(value):
    high = value.astype(BF16)
    return high, (value - high.astype(F32)).astype(BF16)


def wide_dot(left, right, contract):
    return lax.dot_general(left, right, (contract, ((), ())), preferred_element_type=F32)


def phase_rows(orders, count):
    row = lax.broadcasted_iota(jnp.int32, (8, orders.shape[1]), 0)
    fine = 2 * row + 1
    step = jnp.where(row < 4, jnp.left_shift(16, jnp.minimum(row, 4)), (row - 4) * 512 + 256)
    step = jnp.where(row == 7, 1535, step)
    wide = jnp.broadcast_to(orders, (8, orders.shape[1]))
    fine_pair = turn_pair(wide, fine.astype(F32), count)
    step_pair = turn_pair(wide, step.astype(F32), count)
    return fine_pair, step_pair


def fill_tables(fine_pair, step_pair, tables):
    cos_hi, cos_lo, sin_hi, sin_lo = tables
    cosine, sine = fine_pair
    step_cos, step_sin = step_pair
    for level in range(4):
        turn_cos = step_cos[level : level + 1]
        turn_sin = step_sin[level : level + 1]
        next_cos = cosine * turn_cos - sine * turn_sin
        next_sin = sine * turn_cos + cosine * turn_sin
        cosine = jnp.concatenate([cosine, next_cos], axis=0)
        sine = jnp.concatenate([sine, next_sin], axis=0)
    high, low = split(cosine)
    cos_hi[...] = high
    cos_lo[...] = low
    high, low = split(sine)
    sin_hi[...] = high
    sin_lo[...] = low


def reversed_lanes(value):
    index = 127 - lax.broadcasted_iota(jnp.int32, value.shape, 1)
    return jnp.take_along_axis(value, index, axis=1)


def block_swap(parts):
    lane = lax.broadcasted_iota(jnp.int32, parts[0].shape, 1)
    far = lane < 64
    near = (lane // 32) % 2 == 0
    a, b, c, d = parts
    a, c = jnp.where(far, a, pltpu.roll(c, 64, 1)), jnp.where(far, pltpu.roll(a, 64, 1), c)
    b, d = jnp.where(far, b, pltpu.roll(d, 64, 1)), jnp.where(far, pltpu.roll(b, 64, 1), d)
    a, b = jnp.where(near, a, pltpu.roll(b, 32, 1)), jnp.where(near, pltpu.roll(a, 96, 1), b)
    c, d = jnp.where(near, c, pltpu.roll(d, 32, 1)), jnp.where(near, pltpu.roll(c, 96, 1), d)
    return a, b, c, d


def greet_all(barrier, me):
    def greet(k, carry):
        t = lax.rem(me + k, 128)
        pl.semaphore_signal(barrier, inc=1, device_id=(t // 4, lax.rem(t, 4)), device_id_type=MESH)
        return carry

    lax.fori_loop(1, 128, greet, 0)


def partner(k, band, lev):
    step = lax.rem(k * 37, 128)
    y = lax.rem(band // 8 + step // 32, 4)
    x = lax.rem(band // 2 + step // 8, 4)
    core = lax.rem(band + step // 4, 2)
    return y * 8 + x * 2 + core, lax.rem(lev + step, 4)


LIGHT = 15
LOWER = 14
UPPER = 27 - LOWER
HEAVY_DEVICES = (32 - LIGHT) * 4


def post(source, target, chunks, row, place, sems, device):
    pltpu.make_async_remote_copy(
        src_ref=source.at[chunks, pl.ds(row, 1), :],
        dst_ref=target.at[chunks, pl.ds(place, 1), :],
        send_sem=sems.at[0],
        recv_sem=sems.at[1],
        device_id=device,
        device_id_type=MESH,
    ).start()


def drained(source, target, chunks, count, sem, sending, device):
    copy = pltpu.make_async_remote_copy(
        src_ref=source.at[chunks, pl.ds(0, count), :],
        dst_ref=target.at[chunks, pl.ds(0, count), :],
        send_sem=sem,
        recv_sem=sem,
        device_id=device,
        device_id_type=MESH,
    )
    if sending:
        copy.wait_send()
    else:
        copy.wait_recv()


LOW = pl.ds(0, LOWER)
HIGH = pl.ds(LOWER, UPPER)


def wave_orders(pair_slot):
    lanes = jnp.broadcast_to(pair_slot.astype(F32), (128, 384))
    column = jnp.concatenate([lanes[:, 128 * c : 128 * c + 128].T for c in range(3)], axis=0)
    wave = lax.broadcasted_iota(jnp.int32, (384, 128), 0).astype(F32)
    lane = lax.broadcasted_iota(jnp.int32, (384, 128), 1).astype(F32)
    lower = [jnp.sum(jnp.where(column == 3.0 * lane + s, wave, 0.0), axis=0, keepdims=True) for s in range(3)]
    lower = jnp.concatenate(lower, axis=1)
    return jnp.concatenate([lower, 767.0 - lower], axis=1)


def rows_at(member, r, pair, f=0, slot=0):
    return pl.multiple_of(member * 1728 + r * 24 + f * 8 + pair * 144 + slot * 48, 8)


def forward_tables(orders, count, tables):
    fine_pair, step_pair = phase_rows(orders, count)
    fill_tables(fine_pair, step_pair, tables)
    return step_pair


def forward_pair(field, increment, pair, count, weight, orders, tables, steps_ref, rows, spectra):
    for f in range(3):
        for l in range(4):
            at = 8 * f + 2 * l
            rows[at : at + 2, :] = field[f, l, pair] + increment[f, l, pair]
    step_cos, step_sin = forward_tables(orders, count, tables)
    steps_ref[0] = step_cos
    steps_ref[1] = step_sin
    cos_hi, cos_lo, sin_hi, sin_lo = tables
    value = rows[...]
    place = lax.broadcasted_iota(jnp.int32, value.shape, 1).astype(F32)
    value = jnp.where(place < count, value, 0.0)
    even, odd = [], []
    for block in range(6):
        low = reversed_lanes(value[:, 256 * block : 256 * block + 128])
        high = value[:, 256 * block + 128 : 256 * block + 256]
        even.append(high + low)
        odd.append(high - low)

    def folded(parts):
        return jnp.concatenate(
            [parts[3 + g] + parts[2 - g] for g in range(3)] + [parts[3 + g] - parts[2 - g] for g in range(3)],
            axis=0,
        )

    def product(parts, table_hi, table_lo):
        high, low = split(folded(parts))
        both = jnp.concatenate([high, low], axis=1)
        twice = jnp.concatenate([table_hi[...], table_hi[...]], axis=0)
        contract = ((1,), (0,))
        return wide_dot(both, twice, contract) + wide_dot(high, table_lo[...], contract)

    by_cos = product(even, cos_hi, cos_lo)
    by_sin = product(odd, sin_hi, sin_lo)
    real = jnp.zeros((24, 768), F32)
    imag = jnp.zeros((24, 768), F32)
    for g in range(3):
        plus = slice(24 * g, 24 * g + 24)
        minus = slice(72 + 24 * g, 96 + 24 * g)
        turn_cos = step_cos[4 + g : 5 + g]
        turn_sin = step_sin[4 + g : 5 + g]
        real = real + turn_cos * by_cos[plus] - turn_sin * by_sin[minus]
        imag = imag - turn_sin * by_cos[minus] - turn_cos * by_sin[plus]
    live = (2.0 * orders + 1.0 <= count).astype(F32) * (weight / count)
    centre_cos = step_cos[7:8] * live
    centre_sin = step_sin[7:8] * live
    both = (real * centre_cos + imag * centre_sin, imag * centre_cos - real * centre_sin)
    for t in range(6):
        for r in range(2):
            spectra[pl.ds(rows_at(t // 3, r, pair, 0, t % 3), 24), :] = both[r][:, 128 * t : 128 * t + 128]


def inverse_pair(spectra, pair, count, orders, tables, steps_ref, rows, out):
    cos_hi, cos_lo, sin_hi, sin_lo = tables
    step_cos, step_sin = steps_ref[0], steps_ref[1]

    def part(r):
        return jnp.concatenate(
            [spectra[pl.ds(rows_at(t // 3, r, pair, 0, t % 3), 24), :] for t in range(6)], axis=1
        )

    in_real, in_imag = part(0), part(1)
    live = 2.0 * orders + 1.0 <= count
    doubling = jnp.where(live, jnp.where(orders < 0.5, 1.0, 2.0), 0.0)
    centre_cos = step_cos[7:8] * doubling
    centre_sin = step_sin[7:8] * doubling
    real = in_real * centre_cos - in_imag * centre_sin
    imag = in_real * centre_sin + in_imag * centre_cos

    def turned(first, second):
        return jnp.concatenate(
            [first * step_cos[4 + g : 5 + g] for g in range(3)]
            + [second * step_sin[4 + g : 5 + g] for g in range(3)],
            axis=0,
        )

    def product(first, second, table_hi, table_lo):
        high, low = split(turned(first, second))
        contract = ((1,), (1,))
        both = wide_dot(high, jnp.concatenate([table_hi[...], table_lo[...]], axis=0), contract)
        return both[:, :128] + both[:, 128:] + wide_dot(low, table_hi[...], contract)

    by_cos = product(real, imag, cos_hi, cos_lo)
    by_sin = product(imag, real, sin_hi, sin_lo)
    place = lax.broadcasted_iota(jnp.int32, (24, 128), 1).astype(F32)

    def put(block, value):
        rows[:, 128 * block : 128 * block + 128] = jnp.where(place + 128.0 * block < count, value, 0.0)

    for g in range(3):
        c1, c2 = by_cos[24 * g : 24 * g + 24], by_cos[72 + 24 * g : 96 + 24 * g]
        s1, s2 = by_sin[24 * g : 24 * g + 24], by_sin[72 + 24 * g : 96 + 24 * g]
        minus, plus = c1 - c2, c1 + c2
        total, differ = s1 + s2, s1 - s2
        put(2 * (3 + g) + 1, minus - total)
        put(2 * (3 + g), reversed_lanes(minus + total))
        put(2 * (2 - g) + 1, plus - differ)
        put(2 * (2 - g), reversed_lanes(plus + differ))
    for f in range(3):
        for l in range(4):
            at = 8 * f + 2 * l
            out[f, l, pair] = rows[at : at + 2, :]


def prepare_legendre(slot, source, by_lat, by_wave, table_hi, table_lo, last):
    for t in range(3):
        by_lat[t] = source[slot, 0:768, 128 * t : 128 * t + 128]
    for t in range(3):
        for parity in range(2):
            for c in range(3):
                chunk = by_lat[t, pl.ds(256 * c + parity, 128, stride=2), :]
                by_wave[3 * parity + c, 128 * t : 128 * t + 128, :] = chunk.T
        final = jnp.broadcast_to(source[slot, 768:769, 128 * t : 128 * t + 128], (128, 128))
        by_wave[6, 128 * t : 128 * t + 128, :] = final.T
    for i in range(12):
        for c in range(6):
            high, low = split(by_wave[c, pl.ds(i, 32, stride=12), :])
            table_hi[slot, 32 * i : 32 * i + 32, 128 * c : 128 * c + 128] = high
            table_lo[slot, 32 * i : 32 * i + 32, 128 * c : 128 * c + 128] = low
    for t in range(3):
        column = jnp.concatenate([by_wave[6, pl.ds(4 * t + k, 32, stride=12), :] for k in range(4)], axis=0)
        last[slot, :, 128 * t : 128 * t + 128] = column.T[0:8]


def legendre_slot(slot, lower, rates, flat, left, back, table_hi, table_lo, last):
    row = lax.broadcasted_iota(jnp.int32, (8, 128), 0)
    first = row % 2 == 0
    half_lower = lower * 0.5
    odd_lower = lower - 2.0 * jnp.floor(half_lower) > 0.5
    for member in range(2):
        for r in range(2):
            for f in range(3):
                for g in range(3):
                    parts = [flat[pl.ds(rows_at(member, r, 4 * g + k, f, slot), 8), :] for k in range(4)]
                    swapped = block_swap(parts)
                    for z in range(2):
                        a, b = swapped[2 * z], swapped[2 * z + 1]
                        north = jnp.where(first, a, pltpu.roll(b, 1, 0))
                        south = jnp.where(first, pltpu.roll(a, 7, 0), b)
                        plus, minus = north + south, north - south
                        if member:
                            plus, minus = jnp.where(odd_lower, minus, plus), jnp.where(odd_lower, plus, minus)
                        at = (((member * 2 + r) * 2 + z) * 3 + f) * 8
                        left[0, at : at + 8, 128 * g : 128 * g + 128] = plus
                        left[1, at : at + 8, 128 * g : 128 * g + 128] = minus
    lower_row = jnp.concatenate([lower[0:1]] * 3, axis=1)
    for parity in range(2):
        value = left[parity]
        high, low = split(value)
        both = jnp.concatenate([high, low], axis=1)
        cols = slice(384 * parity, 384 * parity + 384)
        hi_table = table_hi[slot, :, cols]
        lo_table = table_lo[slot, :, cols]
        contract = ((1,), (0,))
        coef = wide_dot(both, jnp.concatenate([hi_table, hi_table], axis=0), contract)
        coef = coef + wide_dot(high, lo_table, contract)
        column = 2.0 * lax.broadcasted_iota(jnp.int32, (1, 384), 1).astype(F32) + float(parity)
        second = column >= 768.0 - lower_row
        scales = []
        for member in range(2):
            degree = column - 1.0 if member else lower_row + column
            kept = jnp.where(second, 1.0, 0.0) if member else jnp.where(second, 0.0, 1.0)
            ratio = degree * (degree + 1.0) / float(767 * 768)
            square = ratio * ratio
            scale = jnp.concatenate([kept / (1.0 + rate * square) for rate in rates], axis=0)
            scales += [scale, scale]
        damped = coef * jnp.concatenate(scales, axis=0)
        high, low = split(damped)
        both = jnp.concatenate([high, low], axis=1)
        contract = ((1,), (1,))
        given = wide_dot(both, jnp.concatenate([hi_table, hi_table], axis=1), contract)
        given = given + wide_dot(high, lo_table, contract)
        if parity == 0:
            final = last[slot, 0:1, :]
            extra = jnp.sum(value[96:192] * final, axis=1, keepdims=True)
            fade = jnp.concatenate([1.0 / (1.0 + rate) for rate in rates] * 2, axis=0)
            back[parity, 0:96, :] = given[0:96]
            back[parity, 96:192, :] = given[96:192] + (extra * fade) * final
        else:
            back[parity] = given
    for member in range(2):
        for r in range(2):
            for f in range(3):
                for g in range(3):
                    parts = []
                    for z in range(2):
                        at = (((member * 2 + r) * 2 + z) * 3 + f) * 8
                        plus = back[0, at : at + 8, 128 * g : 128 * g + 128]
                        minus = back[1, at : at + 8, 128 * g : 128 * g + 128]
                        if member:
                            plus, minus = jnp.where(odd_lower, minus, plus), jnp.where(odd_lower, plus, minus)
                        north, south = plus + minus, plus - minus
                        parts.append(jnp.where(first, north, pltpu.roll(south, 1, 0)))
                        parts.append(jnp.where(first, pltpu.roll(north, 7, 0), south))
                    for k, value in enumerate(block_swap(parts)):
                        flat[pl.ds(rows_at(member, r, 4 * g + k, f, slot), 8), :] = value


def step_kernel(
    points, weights, strength, pair_slot, field_hbm, increment_hbm, legendre_hbm, out_hbm,
    field, increment, source, waves, steps, rows, flat, sent, got, left, back, by_lat, by_wave, table_hi, table_lo, last,
    cos_hi_a, cos_lo_a, sin_hi_a, sin_lo_a, cos_hi_b, cos_lo_b, sin_hi_b, sin_lo_b,
    load_sems, low_sems, high_sems, store_sem,
):
    band, lev = lax.axis_index("band"), lax.axis_index("lev")
    me = band * 4 + lev
    here = lev * 32 + band
    device = (band, lev)
    light = band < LIGHT
    loads = [
        pltpu.make_async_copy(field_hbm, field, load_sems.at[0]),
        pltpu.make_async_copy(increment_hbm, increment, load_sems.at[1]),
        pltpu.make_async_copy(legendre_hbm, source, load_sems.at[2]),
    ]
    for load in loads:
        load.start()
    for z in range(4):
        got[0, LOWER:27, 32 * z : 32 * z + LIGHT, :] = jnp.zeros((UPPER, LIGHT, 128), F32)

    @pl.when(light)
    def _():
        got[1, LOWER:27, :, :] = jnp.zeros((UPPER, 128, 128), F32)

    barrier = pltpu.get_barrier_semaphore()
    greet_all(barrier, me)
    waves[...] = wave_orders(pair_slot[...])
    loads[0].wait()
    loads[1].wait()
    table_sets = ((cos_hi_a, cos_lo_a, sin_hi_a, sin_lo_a), (cos_hi_b, cos_lo_b, sin_hi_b, sin_lo_b))

    def forward(k, carry):
        for side in range(2):
            pair = 2 * k + side
            forward_pair(
                field, increment, pair, points[pair].astype(F32), weights[band * 12 + pair], waves[...],
                [table.at[k] for table in table_sets[side]], steps.at[side, k], rows.at[side], flat,
            )
        return carry

    lax.fori_loop(0, 6, forward, 0)
    for c in range(27):
        sent[0, c] = flat[128 * c : 128 * c + 128, :].T
    pl.semaphore_wait(barrier, 127)

    def send_out(k, carry):
        b, z = partner(k, band, lev)
        post(sent.at[0], got.at[0], LOW, b * 4 + z, here, low_sems.at[0], (b, z))

        @pl.when(band >= LIGHT)
        def _():
            post(sent.at[0], got.at[0], HIGH, b * 4 + z, here, high_sems.at[0], (b, z))

        return carry

    lax.fori_loop(1, 128, send_out, 0)
    got[0, :, pl.ds(here, 1), :] = sent[0, :, pl.ds(me, 1), :]
    loads[2].wait()

    def prepare(slot, carry):
        prepare_legendre(slot, source, by_lat, by_wave, table_hi, table_lo, last)
        return carry

    lax.fori_loop(0, 3, prepare, 0)
    rates = []
    for z in range(2):
        for f in range(3):
            index = lax.broadcasted_iota(jnp.int32, (8, 1), 0)
            rate = jnp.zeros((8, 1), F32)
            for l in range(4):
                for side in range(2):
                    rate = jnp.where(index == 2 * l + side, strength[f, 4 * (2 * z + side) + l], rate)
            rates.append(rate)
    drained(sent.at[0], got.at[0], LOW, 127, low_sems.at[0, 1], False, device)

    @pl.when(light)
    def _():
        drained(sent.at[0], got.at[0], HIGH, HEAVY_DEVICES, high_sems.at[0, 1], False, device)

    @pl.when(band >= LIGHT)
    def _():
        drained(sent.at[0], got.at[0], HIGH, HEAVY_DEVICES - 1, high_sems.at[0, 1], False, device)

    for c in range(27):
        flat[128 * c : 128 * c + 128, :] = got[0, c].T
    slots = pair_slot[...].astype(F32)

    def legendre(slot, carry):
        mine = (3 * me + slot).astype(F32)
        index = lax.broadcasted_iota(jnp.int32, (1, 384), 1).astype(F32)
        lower = jnp.sum(jnp.where(slots == mine, index, 0.0), axis=1, keepdims=True)
        lower = jnp.broadcast_to(lower, (8, 128))
        legendre_slot(slot, lower, rates, flat, left, back, table_hi, table_lo, last)
        return carry

    lax.fori_loop(0, 3, legendre, 0)
    for c in range(27):
        sent[1, c] = flat[128 * c : 128 * c + 128, :].T

    def send_back(k, carry):
        b, z = partner(k, band, lev)
        post(sent.at[1], got.at[1], LOW, z * 32 + b, me, low_sems.at[1], (b, z))

        @pl.when(b >= LIGHT)
        def _():
            post(sent.at[1], got.at[1], HIGH, z * 32 + b, me, high_sems.at[1], (b, z))

        return carry

    lax.fori_loop(1, 128, send_back, 0)
    got[1, 0:LOWER, pl.ds(me, 1), :] = sent[1, 0:LOWER, pl.ds(here, 1), :]

    @pl.when(band >= LIGHT)
    def _():
        got[1, LOWER:27, pl.ds(me, 1), :] = sent[1, LOWER:27, pl.ds(here, 1), :]
        drained(sent.at[0], got.at[0], HIGH, 127, high_sems.at[0, 0], True, device)

    drained(sent.at[0], got.at[0], LOW, 127, low_sems.at[0, 0], True, device)
    drained(sent.at[1], got.at[1], LOW, 127, low_sems.at[1, 1], False, device)

    @pl.when(band >= LIGHT)
    def _():
        drained(sent.at[1], got.at[1], HIGH, 127, high_sems.at[1, 1], False, device)

    for c in range(27):
        flat[128 * c : 128 * c + 128, :] = got[1, c].T

    def inverse(k, carry):
        for side in range(2):
            pair = 2 * k + side
            inverse_pair(
                flat, pair, points[pair].astype(F32), waves[...],
                [table.at[k] for table in table_sets[side]], steps.at[side, k], rows.at[side], field,
            )
        return carry

    lax.fori_loop(0, 6, inverse, 0)
    store = pltpu.make_async_copy(field, out_hbm, store_sem)
    store.start()
    drained(sent.at[1], got.at[1], LOW, 127, low_sems.at[1, 0], True, device)

    @pl.when(light)
    def _():
        drained(sent.at[1], got.at[1], HIGH, HEAVY_DEVICES, high_sems.at[1, 0], True, device)

    @pl.when(band >= LIGHT)
    def _():
        drained(sent.at[1], got.at[1], HIGH, HEAVY_DEVICES - 1, high_sems.at[1, 0], True, device)

    store.wait()


ANYWHERE = pl.BlockSpec(memory_space=pl.ANY)
SCALARS = pl.BlockSpec(memory_space=pltpu.SMEM)


def body(field_grid, increment, points, weights, pair_slot, legendre, strength):
    grid = (3, 4, 12, 2, 1536)
    return pl.pallas_call(
        step_kernel,
        out_shape=jax.ShapeDtypeStruct(grid, F32),
        in_specs=[SCALARS, SCALARS, SCALARS, pl.BlockSpec(memory_space=pltpu.VMEM), ANYWHERE, ANYWHERE, ANYWHERE],
        out_specs=ANYWHERE,
        scratch_shapes=[
            pltpu.VMEM(grid, F32),
            pltpu.VMEM(grid, F32),
            pltpu.VMEM((3, 769, 384), F32),
            pltpu.VMEM((1, 768), F32),
            pltpu.VMEM((2, 6, 2, 8, 768), F32),
            pltpu.VMEM((2, 24, 1536), F32),
            pltpu.VMEM((3456, 128), F32),
            pltpu.VMEM((2, 27, 128, 128), F32),
            pltpu.VMEM((2, 27, 128, 128), F32),
            pltpu.VMEM((2, 192, 384), F32),
            pltpu.VMEM((2, 192, 384), F32),
            pltpu.VMEM((3, 768, 128), F32),
            pltpu.VMEM((7, 384, 128), F32),
            pltpu.VMEM((3, 384, 768), BF16),
            pltpu.VMEM((3, 384, 768), BF16),
            pltpu.VMEM((3, 8, 384), F32),
        ]
        + [pltpu.VMEM((6, 128, 768), BF16) for _ in range(8)]
        + [
            pltpu.SemaphoreType.DMA((3,)),
            pltpu.SemaphoreType.DMA((2, 2)),
            pltpu.SemaphoreType.DMA((2, 2)),
            pltpu.SemaphoreType.DMA,
        ],
        compiler_params=pltpu.CompilerParams(
            collective_id=0, has_side_effects=True, vmem_limit_bytes=60 * 1024 * 1024
        ),
        name="spectral_step",
    )(points, weights, strength, pair_slot.reshape(1, 384), field_grid, increment, jnp.swapaxes(legendre, 1, 2))


def solution(mesh):
    return jax.shard_map(
        body,
        mesh=mesh,
        in_specs=(
            P(None, "lev", "band", None, None),
            P(None, "lev", "band", None, None),
            P("band"),
            P(),
            P(),
            P(("band", "lev"), None, None),
            P(),
        ),
        out_specs=P(None, "lev", "band", None, None),
        check_vma=False,
    )
```

time: 126 us -> 78.9 us (0.63); the launches traced: 126 us -> 77.6 us
  Pallas kernels: 118 us -> 73 us
  local copies, waits for them, and re-layouts: 6.92 us -> 4.56 us
  other arithmetic: 1.52 us -> 0 us
    pallas_call x5 -> x1, Pallas kernels: 118 us -> 73 us  [body(): pl.pallas_call(step_kernel, out_shape=jax.ShapeDtypeStruct(grid, F32), in...]
    unnamed x3 -> x1, local copies, waits for them, and re-layouts: 5.36 us -> 3.32 us
where the time goes in v2:
time: 78.9 us; the launch traced here: 77.6 us
  Pallas kernels  73 us (93%)
  local copies, waits for them, and re-layouts  4.56 us (6%)
    pallas_call x1, Pallas kernels, body(): pl.pallas_call(step_kernel, out_shape=jax.ShapeDtypeStruct(grid, F32), in...  73 us
    unnamed x1, local copies, waits for them, and re-layouts  3.32 us

profile of v2, /device:TPU:1, one launch (start us, length us, event | category | flops | bytes accessed | tf_op | source)
XLA Modules:
  0.0 77.6 jit_solution(11660190572201413645)
XLA Ops:
  0.0 1.2 %reshape.3.pair_slot = s32[1,384]{1,0:T(1,128)} reshape(s32[384]{0:T(512)} %param.11) | data formatting | bytes 3072 | tf_op jit(solution)/shard_map/reshape | solution.py:556
  1.2 73.0 %spectral_step.1 = f32[3,4,12,2,1536]{4,3,2,1,0:T(2,128)} custom-call(s32[12]{0:T(128)} %points.1, f32[384]{0:T(512)} %weights.1, f32[3,16]{1,0:T(4,128)} %strength.1, s32[1,384]{1,0:T(1,128)} %reshape.3.pair_slot, f32[3,4,12,2,1536]{4,3,2,1,0:T(2,128)} %field_hbm.1, f32[3,4,12,2,1536]{4,3,2,1,0:T(2,128)} %increment_hbm.1, f32[3,769,384]{2,1,0:T(8,128)} %bitcast.1), custom_call_target="tpu_custom_call" | custom-call | tf_op jit(solution)/shard_map/spectral_step/pallas_call | solution.py:522
  74.3 3.3 %copy.9 = f32[3,4,12,2,1536]{4,3,2,1,0:T(2,128)} copy(f32[3,4,12,2,1536]{4,3,2,1,0:T(2,128)} %spectral_step.1) | data formatting | bytes 3538944

commit v3 on v2

--- a/solution.py
+++ b/solution.py
@@ -53,8 +53,7 @@
     return fine_pair, step_pair
 
 
-def fill_tables(fine_pair, step_pair, tables):
-    cos_hi, cos_lo, sin_hi, sin_lo = tables
+def fill_tables(fine_pair, step_pair, tables, index):
     cosine, sine = fine_pair
     step_cos, step_sin = step_pair
     for level in range(4):
@@ -64,12 +63,10 @@
         next_sin = sine * turn_cos + cosine * turn_sin
         cosine = jnp.concatenate([cosine, next_cos], axis=0)
         sine = jnp.concatenate([sine, next_sin], axis=0)
-    high, low = split(cosine)
-    cos_hi[...] = high
-    cos_lo[...] = low
-    high, low = split(sine)
-    sin_hi[...] = high
-    sin_lo[...] = low
+    for n, value in enumerate((cosine, sine)):
+        high, low = split(value)
+        tables[(*index, 2 * n)] = high
+        tables[(*index, 2 * n + 1)] = low
 
 
 def reversed_lanes(value):
@@ -98,18 +95,15 @@
     lax.fori_loop(1, 128, greet, 0)
 
 
-def partner(k, band, lev):
-    step = lax.rem(k * 37, 128)
-    y = lax.rem(band // 8 + step // 32, 4)
-    x = lax.rem(band // 2 + step // 8, 4)
-    core = lax.rem(band + step // 4, 2)
-    return y * 8 + x * 2 + core, lax.rem(lev + step, 4)
-
-
 LIGHT = 15
-LOWER = 14
-UPPER = 27 - LOWER
-HEAVY_DEVICES = (32 - LIGHT) * 4
+ALL = 9
+LOWER = 5
+HEAVY = (32 - LIGHT) * 4
+SIDES = 4
+
+
+def chunks_of(slot, count):
+    return pl.ds(ALL * slot, count)
 
 
 def post(source, target, chunks, row, place, sems, device):
@@ -123,23 +117,32 @@
     ).start()
 
 
-def drained(source, target, chunks, count, sem, sending, device):
-    copy = pltpu.make_async_remote_copy(
-        src_ref=source.at[chunks, pl.ds(0, count), :],
-        dst_ref=target.at[chunks, pl.ds(0, count), :],
-        send_sem=sem,
-        recv_sem=sem,
-        device_id=device,
-        device_id_type=MESH,
-    )
-    if sending:
-        copy.wait_send()
-    else:
-        copy.wait_recv()
-
-
-LOW = pl.ds(0, LOWER)
-HIGH = pl.ds(LOWER, UPPER)
+def drained(ref, count, sem):
+    pltpu.make_async_copy(ref.at[pl.ds(0, count), :], ref.at[pl.ds(0, count), :], sem).wait()
+
+
+def to_everyone(band, lev, send):
+    y, x, core = band // 8, (band // 2) % 4, band % 2
+    cores = [core, 1 - core]
+    levs = [lax.rem(lev + n, 4) for n in range(4)]
+
+    def some(t, carry):
+        ys = [lax.rem(y + lax.div(t, 4) + n, 4) for n in range(4)]
+        xs = [lax.rem(x + lax.rem(t, 4) + n, 4) for n in range(4)]
+        for n in range(8):
+            b = ys[n % 4] * 8 + xs[n // 2] * 2 + cores[n // 4]
+            z = levs[n % 4]
+            if n == 0:
+
+                @pl.when(t > 0)
+                def _():
+                    send(b, z)
+
+            else:
+                send(b, z)
+        return carry
+
+    lax.fori_loop(0, 16, some, 0)
 
 
 def wave_orders(pair_slot):
@@ -148,29 +151,18 @@
     wave = lax.broadcasted_iota(jnp.int32, (384, 128), 0).astype(F32)
     lane = lax.broadcasted_iota(jnp.int32, (384, 128), 1).astype(F32)
     lower = [jnp.sum(jnp.where(column == 3.0 * lane + s, wave, 0.0), axis=0, keepdims=True) for s in range(3)]
-    lower = jnp.concatenate(lower, axis=1)
-    return jnp.concatenate([lower, 767.0 - lower], axis=1)
+    return [jnp.concatenate([value, 767.0 - value], axis=1) for value in lower]
 
 
 def rows_at(member, r, pair, f=0, slot=0):
-    return pl.multiple_of(member * 1728 + r * 24 + f * 8 + pair * 144 + slot * 48, 8)
-
-
-def forward_tables(orders, count, tables):
-    fine_pair, step_pair = phase_rows(orders, count)
-    fill_tables(fine_pair, step_pair, tables)
-    return step_pair
-
-
-def forward_pair(field, increment, pair, count, weight, orders, tables, steps_ref, rows, spectra):
+    return pl.multiple_of(member * 576 + r * 24 + f * 8 + pair * 48 + slot * 1152, 8)
+
+
+def fold_pair(field, increment, pair, count, rows, folds, index):
     for f in range(3):
         for l in range(4):
             at = 8 * f + 2 * l
             rows[at : at + 2, :] = field[f, l, pair] + increment[f, l, pair]
-    step_cos, step_sin = forward_tables(orders, count, tables)
-    steps_ref[0] = step_cos
-    steps_ref[1] = step_sin
-    cos_hi, cos_lo, sin_hi, sin_lo = tables
     value = rows[...]
     place = lax.broadcasted_iota(jnp.int32, value.shape, 1).astype(F32)
     value = jnp.where(place < count, value, 0.0)
@@ -180,24 +172,34 @@
         high = value[:, 256 * block + 128 : 256 * block + 256]
         even.append(high + low)
         odd.append(high - low)
-
-    def folded(parts):
-        return jnp.concatenate(
+    for n, parts in enumerate((even, odd)):
+        whole = jnp.concatenate(
             [parts[3 + g] + parts[2 - g] for g in range(3)] + [parts[3 + g] - parts[2 - g] for g in range(3)],
             axis=0,
         )
-
-    def product(parts, table_hi, table_lo):
-        high, low = split(folded(parts))
-        both = jnp.concatenate([high, low], axis=1)
-        twice = jnp.concatenate([table_hi[...], table_hi[...]], axis=0)
+        high, low = split(whole)
+        folds[index, n, :, 0:128] = high
+        folds[index, n, :, 128:256] = low
+
+
+def forward_pair(slot, k, folds, pair, count, weight, orders, tables, steps, flat):
+    fine_pair, step_pair = phase_rows(orders, count)
+    fill_tables(fine_pair, step_pair, tables, (slot, k))
+    step_cos, step_sin = step_pair
+    steps[slot, k, 0] = step_cos
+    steps[slot, k, 1] = step_sin
+
+    def product(n):
+        both = folds[k, n]
+        table_hi, table_lo = tables[slot, k, 2 * n], tables[slot, k, 2 * n + 1]
         contract = ((1,), (0,))
-        return wide_dot(both, twice, contract) + wide_dot(high, table_lo[...], contract)
-
-    by_cos = product(even, cos_hi, cos_lo)
-    by_sin = product(odd, sin_hi, sin_lo)
-    real = jnp.zeros((24, 768), F32)
-    imag = jnp.zeros((24, 768), F32)
+        twice = jnp.concatenate([table_hi, table_hi], axis=0)
+        return wide_dot(both, twice, contract) + wide_dot(both[:, 0:128], table_lo, contract)
+
+    by_cos = product(0)
+    by_sin = product(1)
+    real = jnp.zeros((24, 256), F32)
+    imag = jnp.zeros((24, 256), F32)
     for g in range(3):
         plus = slice(24 * g, 24 * g + 24)
         minus = slice(72 + 24 * g, 96 + 24 * g)
@@ -209,18 +211,17 @@
     centre_cos = step_cos[7:8] * live
     centre_sin = step_sin[7:8] * live
     both = (real * centre_cos + imag * centre_sin, imag * centre_cos - real * centre_sin)
-    for t in range(6):
+    for member in range(2):
         for r in range(2):
-            spectra[pl.ds(rows_at(t // 3, r, pair, 0, t % 3), 24), :] = both[r][:, 128 * t : 128 * t + 128]
-
-
-def inverse_pair(spectra, pair, count, orders, tables, steps_ref, rows, out):
-    cos_hi, cos_lo, sin_hi, sin_lo = tables
-    step_cos, step_sin = steps_ref[0], steps_ref[1]
+            flat[pl.ds(rows_at(member, r, pair, 0, slot), 24), :] = both[r][:, 128 * member : 128 * member + 128]
+
+
+def inverse_pair(slot, k, flat, pair, count, orders, tables, steps, sums):
+    step_cos, step_sin = steps[slot, k, 0], steps[slot, k, 1]
 
     def part(r):
         return jnp.concatenate(
-            [spectra[pl.ds(rows_at(t // 3, r, pair, 0, t % 3), 24), :] for t in range(6)], axis=1
+            [flat[pl.ds(rows_at(member, r, pair, 0, slot), 24), :] for member in range(2)], axis=1
         )
 
     in_real, in_imag = part(0), part(1)
@@ -238,14 +239,21 @@
             axis=0,
         )
 
-    def product(first, second, table_hi, table_lo):
+    def product(first, second, n):
         high, low = split(turned(first, second))
         contract = ((1,), (1,))
-        both = wide_dot(high, jnp.concatenate([table_hi[...], table_lo[...]], axis=0), contract)
-        return both[:, :128] + both[:, 128:] + wide_dot(low, table_hi[...], contract)
-
-    by_cos = product(real, imag, cos_hi, cos_lo)
-    by_sin = product(imag, real, sin_hi, sin_lo)
+        table_hi, table_lo = tables[slot, k, 2 * n], tables[slot, k, 2 * n + 1]
+        both = wide_dot(high, jnp.concatenate([table_hi, table_lo], axis=0), contract)
+        return both[:, :128] + both[:, 128:] + wide_dot(low, table_hi, contract)
+
+    by_cos = product(real, imag, 0)
+    by_sin = product(imag, real, 1)
+    sums[k, 0] = sums[k, 0] + by_cos
+    sums[k, 1] = sums[k, 1] + by_sin
+
+
+def unfold_pair(k, pair, count, sums, rows, out):
+    by_cos, by_sin = sums[k, 0], sums[k, 1]
     place = lax.broadcasted_iota(jnp.int32, (24, 128), 1).astype(F32)
 
     def put(block, value):
@@ -362,15 +370,20 @@
 
 def step_kernel(
     points, weights, strength, pair_slot, field_hbm, increment_hbm, legendre_hbm, out_hbm,
-    field, increment, source, waves, steps, rows, flat, sent, got, left, back, by_lat, by_wave, table_hi, table_lo, last,
-    cos_hi_a, cos_lo_a, sin_hi_a, sin_lo_a, cos_hi_b, cos_lo_b, sin_hi_b, sin_lo_b,
-    load_sems, low_sems, high_sems, store_sem,
+    field, increment, source, waves, flat, sent, got, left, back, by_lat, by_wave, table_hi, table_lo, last,
+    rows_0, rows_1, rows_2, rows_3, folds_0, folds_1, folds_2, folds_3, sums_0, sums_1, sums_2, sums_3,
+    steps_0, steps_1, steps_2, steps_3, tables_0, tables_1, tables_2, tables_3,
+    load_sems, sems, store_sem,
 ):
+    rows = (rows_0, rows_1, rows_2, rows_3)
+    folds = (folds_0, folds_1, folds_2, folds_3)
+    sums = (sums_0, sums_1, sums_2, sums_3)
+    steps = (steps_0, steps_1, steps_2, steps_3)
+    tables = (tables_0, tables_1, tables_2, tables_3)
     band, lev = lax.axis_index("band"), lax.axis_index("lev")
     me = band * 4 + lev
     here = lev * 32 + band
-    device = (band, lev)
-    light = band < LIGHT
+    light, heavy = band < LIGHT, band >= LIGHT
     loads = [
         pltpu.make_async_copy(field_hbm, field, load_sems.at[0]),
         pltpu.make_async_copy(increment_hbm, increment, load_sems.at[1]),
@@ -378,46 +391,68 @@
     ]
     for load in loads:
         load.start()
-    for z in range(4):
-        got[0, LOWER:27, 32 * z : 32 * z + LIGHT, :] = jnp.zeros((UPPER, LIGHT, 128), F32)
+    for slot in range(3):
+        for z in range(4):
+            got[0, ALL * slot + LOWER : ALL * slot + ALL, 32 * z : 32 * z + LIGHT, :] = jnp.zeros(
+                (ALL - LOWER, LIGHT, 128), F32
+            )
 
     @pl.when(light)
     def _():
-        got[1, LOWER:27, :, :] = jnp.zeros((UPPER, 128, 128), F32)
+        for slot in range(3):
+            got[1, ALL * slot + LOWER : ALL * slot + ALL, :, :] = jnp.zeros((ALL - LOWER, 128, 128), F32)
 
     barrier = pltpu.get_barrier_semaphore()
     greet_all(barrier, me)
-    waves[...] = wave_orders(pair_slot[...])
+    for slot, value in enumerate(wave_orders(pair_slot[...])):
+        waves[slot] = value
     loads[0].wait()
     loads[1].wait()
-    table_sets = ((cos_hi_a, cos_lo_a, sin_hi_a, sin_lo_a), (cos_hi_b, cos_lo_b, sin_hi_b, sin_lo_b))
-
-    def forward(k, carry):
-        for side in range(2):
-            pair = 2 * k + side
-            forward_pair(
-                field, increment, pair, points[pair].astype(F32), weights[band * 12 + pair], waves[...],
-                [table.at[k] for table in table_sets[side]], steps.at[side, k], rows.at[side], flat,
-            )
+
+    def every(work):
+        def some(k, carry):
+            for side in range(SIDES):
+                pair = SIDES * k + side
+                work(k, side, pair, points[pair].astype(F32))
+            return carry
+
+        lax.fori_loop(0, 12 // SIDES, some, 0)
+
+    def fold(k, side, pair, count):
+        fold_pair(field, increment, pair, count, rows[side], folds[side], k)
+        sums[side][k] = jnp.zeros((2, 144, 128), F32)
+
+    every(fold)
+
+    def outward(slot, carry):
+        def transform(k, side, pair, count):
+            weight = weights[band * 12 + pair]
+            forward_pair(slot, k, folds[side], pair, count, weight, waves[slot], tables[side], steps[side], flat)
+
+        every(transform)
+        for c in range(ALL):
+            chunk = ALL * slot + c
+            sent[0, chunk] = flat[pl.ds(pl.multiple_of(128 * chunk, 128), 128), :].T
+
+        @pl.when(slot == 0)
+        def _():
+            pl.semaphore_wait(barrier, 127)
+
+        for kind, count in ((light, LOWER), (heavy, ALL)):
+
+            @pl.when(kind)
+            def _():
+                def send(b, z):
+                    post(sent.at[0], got.at[0], chunks_of(slot, count), b * 4 + z, here, sems.at[0, slot], (b, z))
+
+                to_everyone(band, lev, send)
+
+        for c in range(ALL):
+            chunk = ALL * slot + c
+            got[0, chunk, pl.ds(here, 1), :] = sent[0, chunk, pl.ds(me, 1), :]
         return carry
 
-    lax.fori_loop(0, 6, forward, 0)
-    for c in range(27):
-        sent[0, c] = flat[128 * c : 128 * c + 128, :].T
-    pl.semaphore_wait(barrier, 127)
-
-    def send_out(k, carry):
-        b, z = partner(k, band, lev)
-        post(sent.at[0], got.at[0], LOW, b * 4 + z, here, low_sems.at[0], (b, z))
-
-        @pl.when(band >= LIGHT)
-        def _():
-            post(sent.at[0], got.at[0], HIGH, b * 4 + z, here, high_sems.at[0], (b, z))
-
-        return carry
-
-    lax.fori_loop(1, 128, send_out, 0)
-    got[0, :, pl.ds(here, 1), :] = sent[0, :, pl.ds(me, 1), :]
+    lax.fori_loop(0, 3, outward, 0)
     loads[2].wait()
 
     def prepare(slot, carry):
@@ -434,82 +469,93 @@
                 for side in range(2):
                     rate = jnp.where(index == 2 * l + side, strength[f, 4 * (2 * z + side) + l], rate)
             rates.append(rate)
-    drained(sent.at[0], got.at[0], LOW, 127, low_sems.at[0, 1], False, device)
-
-    @pl.when(light)
-    def _():
-        drained(sent.at[0], got.at[0], HIGH, HEAVY_DEVICES, high_sems.at[0, 1], False, device)
-
-    @pl.when(band >= LIGHT)
-    def _():
-        drained(sent.at[0], got.at[0], HIGH, HEAVY_DEVICES - 1, high_sems.at[0, 1], False, device)
-
-    for c in range(27):
-        flat[128 * c : 128 * c + 128, :] = got[0, c].T
     slots = pair_slot[...].astype(F32)
 
-    def legendre(slot, carry):
+    def owned(slot, carry):
+        @pl.when(light)
+        def _():
+            drained(flat, (127 - HEAVY) * LOWER + HEAVY * ALL, sems.at[0, slot, 1])
+
+        @pl.when(heavy)
+        def _():
+            drained(flat, (128 - HEAVY) * LOWER + (HEAVY - 1) * ALL, sems.at[0, slot, 1])
+
+        for c in range(ALL):
+            chunk = ALL * slot + c
+            flat[pl.ds(pl.multiple_of(128 * chunk, 128), 128), :] = got[0, chunk].T
         mine = (3 * me + slot).astype(F32)
         index = lax.broadcasted_iota(jnp.int32, (1, 384), 1).astype(F32)
         lower = jnp.sum(jnp.where(slots == mine, index, 0.0), axis=1, keepdims=True)
         lower = jnp.broadcast_to(lower, (8, 128))
         legendre_slot(slot, lower, rates, flat, left, back, table_hi, table_lo, last)
+        for c in range(ALL):
+            chunk = ALL * slot + c
+            sent[1, chunk] = flat[pl.ds(pl.multiple_of(128 * chunk, 128), 128), :].T
+
+        def send(b, z):
+            for kind, count in ((b < LIGHT, LOWER), (b >= LIGHT, ALL)):
+
+                @pl.when(kind)
+                def _():
+                    post(sent.at[1], got.at[1], chunks_of(slot, count), z * 32 + b, me, sems.at[1, slot], (b, z))
+
+        to_everyone(band, lev, send)
+        for c in range(LOWER):
+            chunk = ALL * slot + c
+            got[1, chunk, pl.ds(me, 1), :] = sent[1, chunk, pl.ds(here, 1), :]
+
+        @pl.when(heavy)
+        def _():
+            for c in range(LOWER, ALL):
+                chunk = ALL * slot + c
+                got[1, chunk, pl.ds(me, 1), :] = sent[1, chunk, pl.ds(here, 1), :]
+
         return carry
 
-    lax.fori_loop(0, 3, legendre, 0)
-    for c in range(27):
-        sent[1, c] = flat[128 * c : 128 * c + 128, :].T
-
-    def send_back(k, carry):
-        b, z = partner(k, band, lev)
-        post(sent.at[1], got.at[1], LOW, z * 32 + b, me, low_sems.at[1], (b, z))
-
-        @pl.when(b >= LIGHT)
-        def _():
-            post(sent.at[1], got.at[1], HIGH, z * 32 + b, me, high_sems.at[1], (b, z))
-
+    lax.fori_loop(0, 3, owned, 0)
+
+    def homeward(slot, carry):
+        @pl.when(light)
+        def _():
+            drained(flat, 127 * LOWER, sems.at[1, slot, 1])
+
+        @pl.when(heavy)
+        def _():
+            drained(flat, 127 * ALL, sems.at[1, slot, 1])
+
+        for c in range(ALL):
+            chunk = ALL * slot + c
+            flat[pl.ds(pl.multiple_of(128 * chunk, 128), 128), :] = got[1, chunk].T
+
+        def transform(k, side, pair, count):
+            inverse_pair(slot, k, flat, pair, count, waves[slot], tables[side], steps[side], sums[side])
+
+        every(transform)
         return carry
 
-    lax.fori_loop(1, 128, send_back, 0)
-    got[1, 0:LOWER, pl.ds(me, 1), :] = sent[1, 0:LOWER, pl.ds(here, 1), :]
-
-    @pl.when(band >= LIGHT)
-    def _():
-        got[1, LOWER:27, pl.ds(me, 1), :] = sent[1, LOWER:27, pl.ds(here, 1), :]
-        drained(sent.at[0], got.at[0], HIGH, 127, high_sems.at[0, 0], True, device)
-
-    drained(sent.at[0], got.at[0], LOW, 127, low_sems.at[0, 0], True, device)
-    drained(sent.at[1], got.at[1], LOW, 127, low_sems.at[1, 1], False, device)
-
-    @pl.when(band >= LIGHT)
-    def _():
-        drained(sent.at[1], got.at[1], HIGH, 127, high_sems.at[1, 1], False, device)
-
-    for c in range(27):
-        flat[128 * c : 128 * c + 128, :] = got[1, c].T
-
-    def inverse(k, carry):
-        for side in range(2):
-            pair = 2 * k + side
-            inverse_pair(
-                flat, pair, points[pair].astype(F32), waves[...],
-                [table.at[k] for table in table_sets[side]], steps.at[side, k], rows.at[side], field,
-            )
-        return carry
-
-    lax.fori_loop(0, 6, inverse, 0)
+    lax.fori_loop(0, 3, homeward, 0)
+
+    def unfold(k, side, pair, count):
+        unfold_pair(k, pair, count, sums[side], rows[side], field)
+
+    every(unfold)
     store = pltpu.make_async_copy(field, out_hbm, store_sem)
     store.start()
-    drained(sent.at[1], got.at[1], LOW, 127, low_sems.at[1, 0], True, device)
-
-    @pl.when(light)
-    def _():
-        drained(sent.at[1], got.at[1], HIGH, HEAVY_DEVICES, high_sems.at[1, 0], True, device)
-
-    @pl.when(band >= LIGHT)
-    def _():
-        drained(sent.at[1], got.at[1], HIGH, HEAVY_DEVICES - 1, high_sems.at[1, 0], True, device)
-
+
+    def finish(slot, carry):
+        @pl.when(light)
+        def _():
+            drained(flat, 127 * LOWER, sems.at[0, slot, 0])
+            drained(flat, (127 - HEAVY) * LOWER + HEAVY * ALL, sems.at[1, slot, 0])
+
+        @pl.when(heavy)
+        def _():
+            drained(flat, 127 * ALL, sems.at[0, slot, 0])
+            drained(flat, (128 - HEAVY) * LOWER + (HEAVY - 1) * ALL, sems.at[1, slot, 0])
+
+        return carry
+
+    lax.fori_loop(0, 3, finish, 0)
     store.wait()
 
 
@@ -519,6 +565,7 @@
 
 def body(field_grid, increment, points, weights, pair_slot, legendre, strength):
     grid = (3, 4, 12, 2, 1536)
+    each = 12 // SIDES
     return pl.pallas_call(
         step_kernel,
         out_shape=jax.ShapeDtypeStruct(grid, F32),
@@ -528,9 +575,7 @@
             pltpu.VMEM(grid, F32),
             pltpu.VMEM(grid, F32),
             pltpu.VMEM((3, 769, 384), F32),
-            pltpu.VMEM((1, 768), F32),
-            pltpu.VMEM((2, 6, 2, 8, 768), F32),
-            pltpu.VMEM((2, 24, 1536), F32),
+            pltpu.VMEM((3, 1, 256), F32),
             pltpu.VMEM((3456, 128), F32),
             pltpu.VMEM((2, 27, 128, 128), F32),
             pltpu.VMEM((2, 27, 128, 128), F32),
@@ -542,11 +587,14 @@
             pltpu.VMEM((3, 384, 768), BF16),
             pltpu.VMEM((3, 8, 384), F32),
         ]
-        + [pltpu.VMEM((6, 128, 768), BF16) for _ in range(8)]
+        + [pltpu.VMEM((24, 1536), F32)] * SIDES
+        + [pltpu.VMEM((each, 2, 144, 256), BF16)] * SIDES
+        + [pltpu.VMEM((each, 2, 144, 128), F32)] * SIDES
+        + [pltpu.VMEM((3, each, 2, 8, 256), F32)] * SIDES
+        + [pltpu.VMEM((3, each, 4, 128, 256), BF16)] * SIDES
         + [
             pltpu.SemaphoreType.DMA((3,)),
-            pltpu.SemaphoreType.DMA((2, 2)),
-            pltpu.SemaphoreType.DMA((2, 2)),
+            pltpu.SemaphoreType.DMA((2, 3, 2)),
             pltpu.SemaphoreType.DMA,
         ],
         compiler_params=pltpu.CompilerParams(

time: 78.9 us -> 61.3 us (0.78)
  Pallas kernels: 73 us -> 55.9 us
    pallas_call x1, Pallas kernels: 73 us -> 55.9 us  [body(): pl.pallas_call(step_kernel, out_shape=jax.ShapeDtypeStruct(grid, F32), in...]
where the time goes in v3:
time: 61.3 us; the launch traced here: 60.5 us
  Pallas kernels  55.9 us (91%)
  local copies, waits for them, and re-layouts  4.56 us (7%)
    pallas_call x1, Pallas kernels, body(): pl.pallas_call(step_kernel, out_shape=jax.ShapeDtypeStruct(grid, F32), in...  55.9 us
    unnamed x1, local copies, waits for them, and re-layouts  3.32 us
    reshape x1, local copies, waits for them, and re-layouts, body(): pair_slot.reshape(1, 384)  1.24 us

profile of v3, /device:TPU:1, one launch (start us, length us, event | category | flops | bytes accessed | tf_op | source)
XLA Modules:
  0.0 60.5 jit_solution(16646389053315335080)
XLA Ops:
  0.0 1.2 %reshape.3.pair_slot = s32[1,384]{1,0:T(1,128)} reshape(s32[384]{0:T(512)} %param.11) | data formatting | bytes 3072 | tf_op jit(solution)/shard_map/reshape | solution.py:604
  1.2 55.9 %spectral_step.1 = f32[3,4,12,2,1536]{4,3,2,1,0:T(2,128)} custom-call(s32[12]{0:T(128)} %points.1, f32[384]{0:T(512)} %weights.1, f32[3,16]{1,0:T(4,128)} %strength.1, s32[1,384]{1,0:T(1,128)} %reshape.3.pair_slot, f32[3,4,12,2,1536]{4,3,2,1,0:T(2,128)} %field_hbm.1, f32[3,4,12,2,1536]{4,3,2,1,0:T(2,128)} %increment_hbm.1, f32[3,769,384]{2,1,0:T(8,128)} %bitcast.1), custom_call_target="tpu_custom_call" | custom-call | tf_op jit(solution)/shard_map/spectral_step/pallas_call | solution.py:569
  57.2 3.3 %copy.9 = f32[3,4,12,2,1536]{4,3,2,1,0:T(2,128)} copy(f32[3,4,12,2,1536]{4,3,2,1,0:T(2,128)} %spectral_step.1) | data formatting | bytes 3538944

commit v4 on v3

--- a/solution.py
+++ b/solution.py
@@ -145,8 +145,50 @@
     lax.fori_loop(0, 16, some, 0)
 
 
+def to_everyone_home(band, lev, send):
+    y, x, core = band // 8, (band // 2) % 4, band % 2
+    cores = [core, 1 - core]
+    levs = [lax.rem(lev + n, 4) for n in range(4)]
+
+    def some(t, carry):
+        flip = lax.rem(y + t, 2)
+        xs = [lax.rem(x + lax.div(t, 2) + n, 4) for n in range(4)]
+        for n in range(8):
+            z = levs[n % 4]
+            side = flip if n % 2 == 0 else 1 - flip
+            b = side * 8 + xs[(n // 2 + 2) % 4] * 2 + cores[n // 4]
+            b_heavy = (3 - side) * 8 + xs[n // 2] * 2 + cores[n // 4]
+            self_heavy = (b_heavy == band) & (z == lev)
+            self_light = (b == band) & (z == lev)
+            if n == 0:
+
+                @pl.when(jnp.logical_not(self_heavy))
+                def _():
+                    send(b_heavy, z, ALL)
+
+                @pl.when(jnp.logical_not(self_light | (b == LIGHT)))
+                def _():
+                    send(b, z, LOWER)
+
+            else:
+                send(b_heavy, z, ALL)
+
+                @pl.when(b != LIGHT)
+                def _():
+                    send(b, z, LOWER)
+
+        return carry
+
+    lax.fori_loop(0, 8, some, 0)
+    for z in levs:
+
+        @pl.when(jnp.logical_not((band == LIGHT) & (z == lev)))
+        def _():
+            send(LIGHT, z, ALL)
+
+
 def wave_orders(pair_slot):
-    lanes = jnp.broadcast_to(pair_slot.astype(F32), (128, 384))
+    lanes = jnp.broadcast_to(pair_slot, (128, 384))
     column = jnp.concatenate([lanes[:, 128 * c : 128 * c + 128].T for c in range(3)], axis=0)
     wave = lax.broadcasted_iota(jnp.int32, (384, 128), 0).astype(F32)
     lane = lax.broadcasted_iota(jnp.int32, (384, 128), 1).astype(F32)
@@ -252,12 +294,16 @@
     sums[k, 1] = sums[k, 1] + by_sin
 
 
-def unfold_pair(k, pair, count, sums, rows, out):
+def unfold_pair(k, pair, count, sums, grid):
     by_cos, by_sin = sums[k, 0], sums[k, 1]
     place = lax.broadcasted_iota(jnp.int32, (24, 128), 1).astype(F32)
 
     def put(block, value):
-        rows[:, 128 * block : 128 * block + 128] = jnp.where(place + 128.0 * block < count, value, 0.0)
+        value = jnp.where(place + 128.0 * block < count, value, 0.0)
+        for f in range(3):
+            for l in range(4):
+                at = 8 * f + 2 * l
+                grid[f, l, pair, :, 128 * block : 128 * block + 128] = value[at : at + 2]
 
     for g in range(3):
         c1, c2 = by_cos[24 * g : 24 * g + 24], by_cos[72 + 24 * g : 96 + 24 * g]
@@ -268,10 +314,19 @@
         put(2 * (3 + g), reversed_lanes(minus + total))
         put(2 * (2 - g) + 1, plus - differ)
         put(2 * (2 - g), reversed_lanes(plus + differ))
-    for f in range(3):
-        for l in range(4):
-            at = 8 * f + 2 * l
-            out[f, l, pair] = rows[at : at + 2, :]
+
+
+def pass_kernel(source, target, held, in_sems, out_sems):
+    parts = [(f, l) for f in range(3) for l in range(4)]
+    takes = [pltpu.make_async_copy(source.at[p], held.at[p], in_sems.at[n]) for n, p in enumerate(parts)]
+    gives = [pltpu.make_async_copy(held.at[p], target.at[p], out_sems.at[n]) for n, p in enumerate(parts)]
+    for take in takes:
+        take.start()
+    for take, give in zip(takes, gives):
+        take.wait()
+        give.start()
+    for give in gives:
+        give.wait()
 
 
 def prepare_legendre(slot, source, by_lat, by_wave, table_hi, table_lo, last):
@@ -371,9 +426,9 @@
 def step_kernel(
     points, weights, strength, pair_slot, field_hbm, increment_hbm, legendre_hbm, out_hbm,
     field, increment, source, waves, flat, sent, got, left, back, by_lat, by_wave, table_hi, table_lo, last,
-    rows_0, rows_1, rows_2, rows_3, folds_0, folds_1, folds_2, folds_3, sums_0, sums_1, sums_2, sums_3,
+    grid, rows_0, rows_1, rows_2, rows_3, folds_0, folds_1, folds_2, folds_3, sums_0, sums_1, sums_2, sums_3,
     steps_0, steps_1, steps_2, steps_3, tables_0, tables_1, tables_2, tables_3,
-    load_sems, sems, store_sem,
+    load_sems, legendre_sem, sems, store_sem,
 ):
     rows = (rows_0, rows_1, rows_2, rows_3)
     folds = (folds_0, folds_1, folds_2, folds_3)
@@ -384,13 +439,15 @@
     me = band * 4 + lev
     here = lev * 32 + band
     light, heavy = band < LIGHT, band >= LIGHT
-    loads = [
-        pltpu.make_async_copy(field_hbm, field, load_sems.at[0]),
-        pltpu.make_async_copy(increment_hbm, increment, load_sems.at[1]),
-        pltpu.make_async_copy(legendre_hbm, source, load_sems.at[2]),
-    ]
+    loads = []
+    for k in range(12 // SIDES):
+        part = pl.ds(SIDES * k, SIDES)
+        for n, (far, near) in enumerate(((field_hbm, field), (increment_hbm, increment))):
+            loads.append(pltpu.make_async_copy(far.at[:, :, part], near.at[:, :, part], load_sems.at[n, k]))
+    load_legendre = pltpu.make_async_copy(legendre_hbm, source, legendre_sem)
     for load in loads:
         load.start()
+    load_legendre.start()
     for slot in range(3):
         for z in range(4):
             got[0, ALL * slot + LOWER : ALL * slot + ALL, 32 * z : 32 * z + LIGHT, :] = jnp.zeros(
@@ -404,11 +461,9 @@
 
     barrier = pltpu.get_barrier_semaphore()
     greet_all(barrier, me)
-    for slot, value in enumerate(wave_orders(pair_slot[...])):
+    slots = pair_slot[...].reshape(1, 384).astype(F32)
+    for slot, value in enumerate(wave_orders(slots)):
         waves[slot] = value
-    loads[0].wait()
-    loads[1].wait()
-
     def every(work):
         def some(k, carry):
             for side in range(SIDES):
@@ -422,7 +477,13 @@
         fold_pair(field, increment, pair, count, rows[side], folds[side], k)
         sums[side][k] = jnp.zeros((2, 144, 128), F32)
 
-    every(fold)
+    for k in range(12 // SIDES):
+        loads[2 * k].wait()
+        loads[2 * k + 1].wait()
+        for side in range(SIDES):
+            pair = SIDES * k + side
+            fold(k, side, pair, points[pair].astype(F32))
+
 
     def outward(slot, carry):
         def transform(k, side, pair, count):
@@ -453,7 +514,7 @@
         return carry
 
     lax.fori_loop(0, 3, outward, 0)
-    loads[2].wait()
+    load_legendre.wait()
 
     def prepare(slot, carry):
         prepare_legendre(slot, source, by_lat, by_wave, table_hi, table_lo, last)
@@ -469,7 +530,6 @@
                 for side in range(2):
                     rate = jnp.where(index == 2 * l + side, strength[f, 4 * (2 * z + side) + l], rate)
             rates.append(rate)
-    slots = pair_slot[...].astype(F32)
 
     def owned(slot, carry):
         @pl.when(light)
@@ -492,14 +552,10 @@
             chunk = ALL * slot + c
             sent[1, chunk] = flat[pl.ds(pl.multiple_of(128 * chunk, 128), 128), :].T
 
-        def send(b, z):
-            for kind, count in ((b < LIGHT, LOWER), (b >= LIGHT, ALL)):
-
-                @pl.when(kind)
-                def _():
-                    post(sent.at[1], got.at[1], chunks_of(slot, count), z * 32 + b, me, sems.at[1, slot], (b, z))
-
-        to_everyone(band, lev, send)
+        def send(b, z, count):
+            post(sent.at[1], got.at[1], chunks_of(slot, count), z * 32 + b, me, sems.at[1, slot], (b, z))
+
+        to_everyone_home(band, lev, send)
         for c in range(LOWER):
             chunk = ALL * slot + c
             got[1, chunk, pl.ds(me, 1), :] = sent[1, chunk, pl.ds(here, 1), :]
@@ -527,20 +583,26 @@
             chunk = ALL * slot + c
             flat[pl.ds(pl.multiple_of(128 * chunk, 128), 128), :] = got[1, chunk].T
 
-        def transform(k, side, pair, count):
-            inverse_pair(slot, k, flat, pair, count, waves[slot], tables[side], steps[side], sums[side])
-
-        every(transform)
+        def some(k, carry):
+            for side in range(SIDES):
+                pair = SIDES * k + side
+                count = points[pair].astype(F32)
+                inverse_pair(slot, k, flat, pair, count, waves[slot], tables[side], steps[side], sums[side])
+
+            @pl.when(slot == 2)
+            def _():
+                for side in range(SIDES):
+                    pair = SIDES * k + side
+                    unfold_pair(k, pair, points[pair].astype(F32), sums[side], grid)
+                part = pl.ds(SIDES * k, SIDES)
+                pltpu.make_async_copy(grid.at[:, :, part], out_hbm.at[:, :, part], store_sem).start()
+
+            return carry
+
+        lax.fori_loop(0, 12 // SIDES, some, 0)
         return carry
 
     lax.fori_loop(0, 3, homeward, 0)
-
-    def unfold(k, side, pair, count):
-        unfold_pair(k, pair, count, sums[side], rows[side], field)
-
-    every(unfold)
-    store = pltpu.make_async_copy(field, out_hbm, store_sem)
-    store.start()
 
     def finish(slot, carry):
         @pl.when(light)
@@ -556,7 +618,7 @@
         return carry
 
     lax.fori_loop(0, 3, finish, 0)
-    store.wait()
+    pltpu.make_async_copy(grid, out_hbm, store_sem).wait()
 
 
 ANYWHERE = pl.BlockSpec(memory_space=pl.ANY)
@@ -566,7 +628,7 @@
 def body(field_grid, increment, points, weights, pair_slot, legendre, strength):
     grid = (3, 4, 12, 2, 1536)
     each = 12 // SIDES
-    return pl.pallas_call(
+    stepped = pl.pallas_call(
         step_kernel,
         out_shape=jax.ShapeDtypeStruct(grid, F32),
         in_specs=[SCALARS, SCALARS, SCALARS, pl.BlockSpec(memory_space=pltpu.VMEM), ANYWHERE, ANYWHERE, ANYWHERE],
@@ -586,6 +648,7 @@
             pltpu.VMEM((3, 384, 768), BF16),
             pltpu.VMEM((3, 384, 768), BF16),
             pltpu.VMEM((3, 8, 384), F32),
+            pltpu.VMEM(grid, F32),
         ]
         + [pltpu.VMEM((24, 1536), F32)] * SIDES
         + [pltpu.VMEM((each, 2, 144, 256), BF16)] * SIDES
@@ -593,7 +656,8 @@
         + [pltpu.VMEM((3, each, 2, 8, 256), F32)] * SIDES
         + [pltpu.VMEM((3, each, 4, 128, 256), BF16)] * SIDES
         + [
-            pltpu.SemaphoreType.DMA((3,)),
+            pltpu.SemaphoreType.DMA((2, each)),
+            pltpu.SemaphoreType.DMA,
             pltpu.SemaphoreType.DMA((2, 3, 2)),
             pltpu.SemaphoreType.DMA,
         ],
@@ -601,7 +665,15 @@
             collective_id=0, has_side_effects=True, vmem_limit_bytes=60 * 1024 * 1024
         ),
         name="spectral_step",
-    )(points, weights, strength, pair_slot.reshape(1, 384), field_grid, increment, jnp.swapaxes(legendre, 1, 2))
+    )(points, weights, strength, pair_slot, field_grid, increment, jnp.swapaxes(legendre, 1, 2))
+    return pl.pallas_call(
+        pass_kernel,
+        out_shape=jax.ShapeDtypeStruct(grid, F32),
+        in_specs=[ANYWHERE],
+        out_specs=ANYWHERE,
+        scratch_shapes=[pltpu.VMEM(grid, F32), pltpu.SemaphoreType.DMA((12,)), pltpu.SemaphoreType.DMA((12,))],
+        name="pass_on",
+    )(stepped)
 
 
 def solution(mesh):

time: 61.3 us -> 58 us (0.946)
  local copies, waits for them, and re-layouts: 4.56 us -> 0 us
  Pallas kernels: 55.9 us -> 57.7 us
    unnamed x1 -> x0, local copies, waits for them, and re-layouts: 3.32 us -> none
    pallas_call x0 -> x1, Pallas kernels: none -> 2.41 us  [body(): pl.pallas_call(pass_kernel, out_shape=jax.ShapeDtypeStruct(grid, F32), in...]
    reshape x1 -> x0, local copies, waits for them, and re-layouts: 1.24 us -> none  [body(): pair_slot.reshape(1, 384)]
    pallas_call x1, Pallas kernels: 55.9 us -> 55.3 us  [body(): pl.pallas_call(step_kernel, out_shape=jax.ShapeDtypeStruct(grid, F32), in...]
where the time goes in v4:
time: 58 us; the launch traced here: 57.7 us
  Pallas kernels  57.7 us (99%)
    pallas_call x1, Pallas kernels, body(): pl.pallas_call(step_kernel, out_shape=jax.ShapeDtypeStruct(grid, F32), in...  55.3 us
    pallas_call x1, Pallas kernels, body(): pl.pallas_call(pass_kernel, out_shape=jax.ShapeDtypeStruct(grid, F32), in...  2.41 us

profile of v4, /device:TPU:1, one launch (start us, length us, event | category | flops | bytes accessed | tf_op | source)
XLA Modules:
  0.0 57.7 jit_solution(5347268608642674366)
XLA Ops:
  0.0 55.3 %spectral_step.1.source = f32[3,4,12,2,1536]{4,3,2,1,0:T(2,128)} custom-call(s32[12]{0:T(128)} %points.1, f32[384]{0:T(512)} %weights.1, f32[3,16]{1,0:T(4,128)} %strength.1, s32[384]{0:T(512)} %pair_slot.1, f32[3,4,12,2,1536]{4,3,2,1,0:T(2,128)} %field_hbm.1, f32[3,4,12,2,1536]{4,3,2,1,0:T(2,128)} %increment_hbm.1, f32[3,769,384]{2,1,0:T(8,128)} %bitcast.1), custom_call_target="tpu_custom_call" | custom-call | tf_op jit(solution)/shard_map/spectral_step/pallas_call | solution.py:631
  55.3 2.4 %pass_on.1 = f32[3,4,12,2,1536]{4,3,2,1,0:T(2,128)} custom-call(f32[3,4,12,2,1536]{4,3,2,1,0:T(2,128)} %spectral_step.1.source), custom_call_target="tpu_custom_call" | custom-call | tf_op jit(solution)/shard_map/pass_on/pallas_call | solution.py:669

commit v5 on v4

--- a/solution.py
+++ b/solution.py
@@ -127,10 +127,10 @@
     levs = [lax.rem(lev + n, 4) for n in range(4)]
 
     def some(t, carry):
-        ys = [lax.rem(y + lax.div(t, 4) + n, 4) for n in range(4)]
+        there = lax.rem(y + lax.div(t, 4), 4)
         xs = [lax.rem(x + lax.rem(t, 4) + n, 4) for n in range(4)]
         for n in range(8):
-            b = ys[n % 4] * 8 + xs[n // 2] * 2 + cores[n // 4]
+            b = there * 8 + xs[n // 2] * 2 + cores[n // 4]
             z = levs[n % 4]
             if n == 0:
 

time: 58 us -> 57.9 us (level)
  no operation moved by 1% of the time
where the time goes in v5:
time: 57.9 us; the launch traced here: 57.7 us
  Pallas kernels  57.7 us (100%)
    pallas_call x1, Pallas kernels, body(): pl.pallas_call(step_kernel, out_shape=jax.ShapeDtypeStruct(grid, F32), in...  55.3 us
    pallas_call x1, Pallas kernels, body(): pl.pallas_call(pass_kernel, out_shape=jax.ShapeDtypeStruct(grid, F32), in...  2.41 us

profile of v5, /device:TPU:1, one launch (start us, length us, event | category | flops | bytes accessed | tf_op | source)
XLA Modules:
  0.0 57.7 jit_solution(14864761685581875956)
XLA Ops:
  0.0 55.3 %spectral_step.1.source = f32[3,4,12,2,1536]{4,3,2,1,0:T(2,128)} custom-call(s32[12]{0:T(128)} %points.1, f32[384]{0:T(512)} %weights.1, f32[3,16]{1,0:T(4,128)} %strength.1, s32[384]{0:T(512)} %pair_slot.1, f32[3,4,12,2,1536]{4,3,2,1,0:T(2,128)} %field_hbm.1, f32[3,4,12,2,1536]{4,3,2,1,0:T(2,128)} %increment_hbm.1, f32[3,769,384]{2,1,0:T(8,128)} %bitcast.1), custom_call_target="tpu_custom_call" | custom-call | tf_op jit(solution)/shard_map/spectral_step/pallas_call | solution.py:631
  55.3 2.4 %pass_on.1 = f32[3,4,12,2,1536]{4,3,2,1,0:T(2,128)} custom-call(f32[3,4,12,2,1536]{4,3,2,1,0:T(2,128)} %spectral_step.1.source), custom_call_target="tpu_custom_call" | custom-call | tf_op jit(solution)/shard_map/pass_on/pallas_call | solution.py:669
